TPU v7x, 256 devices: a whole 4x4x8 slice. The times are simulated.
256 devices in a mesh: tp: 32 (over z, y), kv: 8 (over x, core).
Axes of the slice: x: 4, y: 4, z: 8, core: 2. Of those that a mesh axis runs over, the one named last changes fastest.
Arguments:
- hidden_in: bfloat16 [2048, 4096], P(('kv', 'tp')), may hold values from -6 to 6
- gain_attn: float32 [4096], replicated, may hold values from 0.4 to 1.6
- w_qkv: bfloat16 [4096, 32, 384], P(None, 'tp'), may hold values from -0.09375 to 0.09375
- cache_kv: bfloat16 [2, 8192, 32, 256], P(None, 'kv', 'tp'), may hold values from -110 to 110
- cache_len: int32 [2], replicated, may hold values from 128 to 8192, as said below
- w_out: bfloat16 [4096, 4096], P('tp'), may hold values from -0.1875 to 0.1875
- gain_mlp: float32 [4096], replicated, may hold values from 0.1 to 1.9
- w_gate_up: bfloat16 [4096, 2, 11008], P('kv', None, 'tp'), may hold values from -0.09375 to 0.09375
- w_down: bfloat16 [11008, 4096], P('tp', 'kv'), may hold values from -0.0546875 to 0.0546875
Outputs:
- layer_out: bfloat16 [2048, 4096], P(('kv', 'tp'))
Inputs may be any that keep to these rules, and one draw needn't show every extreme that they name: `cache_len`: every length is a multiple of 128; some sequence uses the whole cache.
All inputs are finite; a program needn't handle non-finite values.
Results may differ from a plain program's by a relative error of at most 0.019.
The roundings to bfloat16 on the way count: a program that leaves them out, or rounds other values in their place, can miss the bound.
Values may be sent and summed in bfloat16 or wider, within the bound.
No kernel may reach another device: no remote copies, remote signals or barrier semaphores. Data moves between devices by JAX's collectives and lax.ppermute only.
A program may use at most 64 MiB of HBM per device.

v0:
```python
import functools
import math

import jax
import jax.numpy as jnp
from jax import lax
from jax.experimental import pallas as pl
from jax.experimental.pallas import tpu as pltpu
from jax.sharding import Mesh
from jax.sharding import PartitionSpec as P


TP = ("z", "y")
KV = ("x", "c")
KV_TP = ("x", "c", "z", "y")

EPSILON = 1e-05
MASKED = -1e30
LOG2E = 1.4426950408889634
F32 = jnp.float32
BF16 = jnp.bfloat16


def shifted(value, axis, step):
    count = lax.axis_size(axis)
    return lax.ppermute(value, axis, [(i, (i + step) % count) for i in range(count)])


def gathered_turned(value, axis):
    return [value] + [shifted(value, axis, s) for s in range(1, lax.axis_size(axis))]


def dot(a, b, ca, cb):
    return lax.dot_general(a, b, (((ca,), (cb,)), ((), ())), preferred_element_type=F32)


def run(kernel, table, arrays, outs, flops=0, limit=16, scratch=()):
    return pl.pallas_call(
        kernel,
        in_specs=[pl.BlockSpec(memory_space=pltpu.SMEM)]
        + [pl.BlockSpec(memory_space=pltpu.VMEM)] * len(arrays),
        out_specs=[pl.BlockSpec(memory_space=pltpu.VMEM)] * len(outs),
        out_shape=[jax.ShapeDtypeStruct(shape, kind) for shape, kind in outs],
        scratch_shapes=[pltpu.VMEM(shape, kind) for shape, kind in scratch],
        compiler_params=pltpu.CompilerParams(vmem_limit_bytes=limit << 20),
        cost_estimate=pl.CostEstimate(flops=flops, transcendentals=0, bytes_accessed=0),
    )(table, *arrays)


WEIGHTS, BLOCKS, TURN, AHEAD, SEQ, LIMIT, OWN, CORE = range(8)


def table_of_places(cache_len, seqs, spots):
    groups, lanes, sides = lax.axis_size("z"), lax.axis_size("y"), lax.axis_size("x")
    x_at, c_at, z_at, y_at = (lax.axis_index(name) for name in ("x", "c", "z", "y"))
    step = jnp.arange(8, dtype=jnp.int32)
    x_from = (x_at + 2 * sides - step) & (sides - 1)
    seq = x_from // (sides // seqs)
    rows = [None] * 8
    rows[WEIGHTS] = 2 * x_from + ((c_at + step // sides) & 1)
    rows[BLOCKS] = (z_at + groups + (1 - 2 * (step & 1)) * ((step + 1) // 2)) & (groups - 1)
    rows[TURN] = (y_at + 2 * lanes - step) & (lanes - 1)
    rows[AHEAD] = (y_at + step) & (lanes - 1)
    rows[SEQ] = seq
    rows[LIMIT] = jnp.where(seq == 0, cache_len[0], cache_len[1]) - (2 * x_at + c_at) * spots
    rows[OWN] = (seq == x_at // (sides // seqs)).astype(jnp.int32)
    rows[CORE] = c_at + 0 * step
    return jnp.stack(rows)


def rows_of(blocks):
    return sum(block.shape[0] for block in blocks)


def project_rows(x_refs, gain_ref, w_ref):
    steps = 4
    width = w_ref.shape[0] // steps

    def chunk(j):
        cols = pl.ds(pl.multiple_of(j * width, width), width)
        return cols, jnp.concatenate([ref[:, cols] for ref in x_refs], axis=0).astype(F32)

    def squares(j, total):
        _, x = chunk(j)
        return total + jnp.sum(x * x, axis=1, keepdims=True)

    total = lax.fori_loop(0, steps, squares, jnp.zeros((rows_of(x_refs), 1), F32))
    inv = lax.rsqrt(total / w_ref.shape[0] + EPSILON)

    def body(j, acc):
        cols, x = chunk(j)
        return acc + dot((x * inv * gain_ref[:, cols]).astype(BF16), w_ref[cols], 1, 0)

    return lax.fori_loop(0, steps, body, jnp.zeros((rows_of(x_refs), w_ref.shape[1]), F32))


def qkv_first_kernel(table_ref, gain_ref, w_ref, *refs):
    *x_refs, out_ref = refs
    out_ref[...] = project_rows(x_refs, gain_ref, w_ref).astype(BF16)


def qkv_last_kernel(table_ref, gain_ref, w_ref, first_ref, *refs):
    *x_refs, q_ref, k_ref, v_ref = refs
    acc = project_rows(x_refs, gain_ref, w_ref).astype(BF16)
    size = q_ref.shape[1]
    done = first_ref.shape[0]
    for at, ref in enumerate((q_ref, k_ref, v_ref)):
        ref[:done] = first_ref[:, at * size : (at + 1) * size]
        ref[done:] = acc[:, at * size : (at + 1) * size]


def qkv_first(table, blocks, gain, weights):
    depth, packed = weights.shape
    count = rows_of(blocks)
    (out,) = run(
        qkv_first_kernel,
        table,
        [gain, weights, *blocks],
        [((count, packed), BF16)],
        2 * count * depth * packed,
    )
    return out


def qkv_last(table, first, blocks, gain, weights):
    depth, packed = weights.shape
    count = rows_of(blocks)
    return run(
        qkv_last_kernel,
        table,
        [gain, weights, first, *blocks],
        [((count + first.shape[0], packed // 3), BF16)] * 3,
        2 * count * depth * packed,
    )


def split3(value):
    first = value.astype(BF16).astype(F32)
    second = (value - first).astype(BF16).astype(F32)
    return first, second, value - first - second


def stats_of(peak, mass):
    row = lax.broadcasted_iota(jnp.int32, (16, peak.shape[1]), 0)
    stats = jnp.zeros((16, peak.shape[1]), F32)
    for at, part in enumerate(split3(peak) + split3(mass)):
        stats = jnp.where(row == at, part, stats)
    return stats.astype(BF16)


def attend_kernel(slots, table_ref, k_ref, v_ref, cache_ref, *refs):
    *refs, q_buf, out_buf = refs
    q_refs, out_refs = refs[: len(slots)], refs[len(slots) :]
    blocks, size = k_ref.shape
    scale = LOG2E / math.sqrt(size)
    halves = q_buf.shape[1] // blocks
    for at, ref in enumerate(q_refs):
        q_buf[at] = ref[...]

    @pl.loop(0, len(slots) * halves)
    def _(turn):
        which, half = turn // halves, turn % halves
        slot = slots[0] + which * (slots[-1] - slots[0])
        seq = table_ref[SEQ, slot]
        limit = table_ref[LIMIT, slot]
        own = table_ref[OWN, slot] > 0
        at = pl.ds(pl.multiple_of(half * blocks, blocks), blocks)
        q = q_buf[which, at]
        s1 = dot(cache_ref[seq, :, :size], q, 1, 1) * scale
        s2 = dot(k_ref[...], q, 1, 1) * scale
        usable = lax.broadcasted_iota(jnp.int32, s1.shape, 0) < limit
        s1 = jnp.where(usable, s1, MASKED)
        s2 = jnp.where(own, s2, MASKED)
        top = jnp.maximum(jnp.max(s1, axis=0, keepdims=True), jnp.max(s2, axis=0, keepdims=True))
        peak = jnp.maximum(top, 0.1 * MASKED)
        p1 = jnp.exp2(s1 - peak)
        p2 = jnp.exp2(s2 - peak)
        mass = jnp.sum(p1, axis=0, keepdims=True) + jnp.sum(p2, axis=0, keepdims=True)
        acc = dot(cache_ref[seq, :, size:], p1.astype(BF16), 0, 0)
        acc += dot(v_ref[...], p2.astype(BF16), 0, 0)
        out_buf[which, :size, at] = acc.astype(BF16)
        out_buf[which, size:, at] = stats_of(peak, mass)

    for at, ref in enumerate(out_refs):
        ref[...] = out_buf[at]


def attend(table, slots, queries, k, v, cache):
    count, size = k.shape
    rows = queries[0].shape[0]
    return run(
        functools.partial(attend_kernel, slots),
        table,
        [k, v, cache, *queries],
        [((size + 16, rows), BF16)] * len(slots),
        4 * rows_of(queries) * size * (cache.shape[1] + count),
        scratch=[((len(slots), rows, size), BF16), ((len(slots), size + 16, rows), BF16)],
    )


def merged(parts, size):
    stats = [part[size:].astype(F32) for part in parts]
    peaks = [s[0:1] + s[1:2] + s[2:3] for s in stats]
    best = functools.reduce(jnp.maximum, peaks)
    mass = jnp.zeros_like(best)
    acc = jnp.zeros((size, best.shape[1]), F32)
    for part, s, peak in zip(parts, stats, peaks):
        scaling = jnp.exp2(peak - best)
        mass += (s[3:4] + s[4:5] + s[5:6]) * scaling
        acc += part[:size].astype(F32) * scaling
    return best, mass, acc


def merge_kernel(table_ref, *refs):
    *parts, mine_ref, other_ref = refs
    height, width = mine_ref.shape
    size = height - 16
    core = table_ref[CORE, 0]
    for ref, side in ((mine_ref, core), (other_ref, 1 - core)):
        cols = pl.ds(pl.multiple_of(side * width, width), width)
        best, mass, acc = merged([part[:, cols] for part in parts], size)
        ref[:size] = acc.astype(BF16)
        ref[size:] = stats_of(best, mass)


def merge(table, parts):
    height, width = parts[0].shape
    return run(merge_kernel, table, parts, [((height, width // 2), BF16)] * 2)


def combine_kernel(table_ref, mine_ref, other_ref, out_ref):
    size = mine_ref.shape[0] - 16
    lanes, rows, _ = out_ref.shape
    _, mass, acc = merged([mine_ref[...], other_ref[...]], size)
    attended = (acc / mass).T.reshape(rows // 8, lanes, 8, size)
    for s in range(lanes):
        out_ref[table_ref[TURN, s]] = attended[:, s].reshape(rows, size).astype(BF16)


def combine(table, mine, other, lanes):
    height, width = mine.shape
    shape = (lanes, width // lanes, height - 16)
    (out,) = run(combine_kernel, table, [mine, other], [(shape, BF16)])
    return out


def project_kernel(table_ref, heads_ref, *refs):
    *w_refs, out_ref = refs
    groups, rows, width = out_ref.shape
    heads = jnp.concatenate(
        [heads_ref[table_ref[AHEAD, s]] for s in range(len(w_refs))], axis=1
    )
    tile = width // 4

    @pl.loop(0, 4)
    def _(j):
        cols = pl.ds(pl.multiple_of(j * tile, tile), tile)
        acc = dot(heads, jnp.concatenate([w[:, cols] for w in w_refs], axis=0), 1, 0)
        acc = acc.reshape(groups, rows, tile)
        for s in range(groups):
            out_ref[table_ref[BLOCKS, s], :, cols] = acc[s].astype(BF16)


def project(table, heads, weights, groups):
    _, rows, _ = heads.shape
    shape = (groups, rows // groups, weights[0].shape[1])
    (out,) = run(project_kernel, table, [heads, *weights], [(shape, BF16)])
    return out


def residual_kernel(table_ref, terms_ref, hidden_ref, gain_ref, residual_ref, normed_ref):
    total = terms_ref[0].astype(F32)
    for s in range(1, terms_ref.shape[0]):
        total += terms_ref[s].astype(F32)
    total += hidden_ref[...].astype(F32)
    residual_ref[...] = total
    inv = lax.rsqrt(jnp.mean(total * total, axis=1, keepdims=True) + EPSILON)
    normed_ref[...] = (total * inv * gain_ref[...]).astype(BF16)


def add_and_norm(table, terms, hidden, gain):
    outs = [(hidden.shape, F32), (hidden.shape, BF16)]
    return run(residual_kernel, table, [terms, hidden, gain], outs)


def gate_up_kernel(table_ref, near_ref, far_ref, *refs):
    *x_refs, out_ref, sums = refs
    side, _, _, depth = near_ref.shape
    sums[...] = jnp.zeros_like(sums)
    for at, w_ref in enumerate((near_ref, far_ref)):

        @pl.loop(0, side)
        def _(j, at=at, w_ref=w_ref):
            place = table_ref[WEIGHTS, at * side + j]
            cols = pl.ds(pl.multiple_of(place * depth, depth), depth)
            x = jnp.concatenate([ref[:, cols] for ref in x_refs], axis=0)
            sums[0] += dot(w_ref[j, 0], x, 1, 1)
            sums[1] += dot(w_ref[j, 1], x, 1, 1)

    gate = sums[0]
    out_ref[...] = (gate / (1.0 + jnp.exp(-gate)) * sums[1]).T.astype(BF16)


def gate_up(table, blocks, weights):
    count = rows_of(blocks)
    side, _, hidden, depth = weights[0].shape
    (out,) = run(
        gate_up_kernel,
        table,
        [*weights, *blocks],
        [((count, hidden), BF16)],
        8 * count * side * hidden * depth,
        scratch=[((2, hidden, count), F32)],
    )
    return out


def down_kernel(lanes, table_ref, x_ref, *refs):
    w_refs, out_refs = refs[:-lanes], refs[-lanes:]
    rows, side, width = x_ref.shape[0], w_refs[0].shape[0], w_refs[0].shape[2]
    for at, w_ref in enumerate(w_refs):

        @pl.loop(0, side)
        def _(j, at=at, w_ref=w_ref):
            acc = dot(x_ref[...], w_ref[j], 1, 0).reshape(rows // (8 * lanes), lanes, 8, width)
            place = table_ref[WEIGHTS, at * side + j]
            cols = pl.ds(pl.multiple_of(place * width, width), width)
            for s, ref in enumerate(out_refs):
                ref[:, cols] = acc[:, s].reshape(rows // lanes, width).astype(BF16)


def down(table, rows, weights, lanes):
    side, _, width = weights[0].shape
    shape = (rows.shape[0] // lanes, side * width * len(weights))
    return run(
        functools.partial(down_kernel, lanes), table, [rows, *weights], [(shape, BF16)] * lanes
    )


def sum_kernel(table_ref, *refs):
    *ins, out_ref = refs
    total = ins[0][...].astype(F32)
    for ref in ins[1:]:
        total += ref[...].astype(F32)
    groups, rows, width = out_ref.shape
    total = total.reshape(groups, rows, width)
    for s in range(groups):
        out_ref[table_ref[BLOCKS, s]] = total[s].astype(BF16)


def sum_pieces(table, pieces, groups):
    rows, width = pieces[0].shape
    outs = [((groups, rows // groups, width), BF16)]
    (out,) = run(sum_kernel, table, pieces, outs)
    return out


def per_device(
    hidden_in, gain_attn, w_qkv, cache_kv, cache_len, w_out, gain_mlp, w_gate_up, w_down
):
    depth, _, packed = w_qkv.shape
    seqs, spots = cache_kv.shape[:2]
    groups, lanes = lax.axis_size("z"), lax.axis_size("y")
    tied = lax.optimization_barrier
    w_qkv = w_qkv.reshape(depth, packed)
    gain_attn, gain_mlp = gain_attn.reshape(1, depth), gain_mlp.reshape(1, depth)
    cache = cache_kv.reshape(seqs, spots, cache_kv.shape[3])
    table = table_of_places(cache_len, seqs, spots)

    def gather_y(value):
        return tied(jnp.concatenate(gathered_turned(value, "y"), axis=0))

    def along_y(value):
        return [value] + [shifted(value, "y", -s) for s in range(1, lanes)]

    def exchanged(value, axis):
        return lax.all_to_all(value, axis, split_axis=0, concat_axis=0, tiled=True)

    r0 = gather_y(hidden_in)
    r0, w_gate_up, w_out, w_down = tied((r0, w_gate_up.transpose(1, 2, 0), w_out, w_down))
    f1, b1 = shifted(r0, "z", 1), shifted(r0, "z", -1)
    gates = gathered_turned(w_gate_up, "x")
    f2, b2 = shifted(f1, "z", 1), shifted(b1, "z", -1)
    w_heads = along_y(w_out)
    f3, b3 = shifted(f2, "z", 1), shifted(b2, "z", -1)
    f4 = shifted(f3, "z", 1)
    first = qkv_first(table, [r0, f1, b1, f2, b2], gain_attn, w_qkv)
    q, k, v = qkv_last(table, first, [f3, b3, f4], gain_attn, w_qkv)

    q = lax.all_gather(q, "c", axis=0, tiled=True)
    queries = gathered_turned(q, "x")
    parts = list(attend(table, (0,), queries[:1], k, v, cache))
    for slots in ((1, 3), (2,)):
        done = attend(table, slots, [queries[s] for s in slots], k, v, cache)
        parts += [shifted(part, "x", -s) for s, part in zip(slots, done)]
    mine, other = merge(table, parts)
    other = shifted(other, "c", 1)
    attended = combine(table, mine, other, lanes)

    attended, gates = tied((attended, gates))
    gates = jnp.stack(gates)
    gates = [gates, shifted(gates, "c", 1)]
    heads_here = exchanged(attended, "y")
    terms = project(table, heads_here, w_heads, groups)
    downs = gathered_turned(w_down, "x")
    terms = exchanged(terms, "z")
    residual, normed = add_and_norm(table, terms, hidden_in, gain_mlp)
    normed, gates = tied((normed, gates))

    r0 = gather_y(normed)
    f1, b1 = shifted(r0, "z", 1), shifted(r0, "z", -1)
    f2, b2 = shifted(f1, "z", 1), shifted(b1, "z", -1)
    f3, b3 = shifted(f2, "z", 1), shifted(b2, "z", -1)
    f3, downs = tied((f3, downs))
    downs = jnp.stack(downs)
    downs = [downs, shifted(downs, "c", 1)]
    f4 = shifted(f3, "z", 1)
    activated = gate_up(table, [r0, f1, b1, f2, b2, f3, b3, f4], gates)
    pieces = down(table, activated, downs, lanes)
    pieces = [shifted(piece, "y", -s) if s else piece for s, piece in enumerate(pieces)]
    shares = exchanged(sum_pieces(table, pieces, groups), "z")
    return (residual + shares.astype(F32).sum(axis=0)).astype(BF16)


def solution(mesh):
    split = Mesh(mesh.devices.reshape(8, 4, 4, 2), ("z", "y", "x", "c"))
    in_specs = (
        P(KV_TP, None),
        P(),
        P(None, TP, None),
        P(None, KV, TP, None),
        P(),
        P(TP, None),
        P(),
        P(KV, None, TP),
        P(TP, KV),
    )
    return jax.shard_map(
        per_device, mesh=split, in_specs=in_specs, out_specs=P(KV_TP, None), check_vma=False
    )
```

profile of v0, /device:TPU:2, one launch (start us, length us, event | category | flops | bytes accessed | tf_op | source)
XLA Modules:
  0.0 289.6 jit_solution(10050022818583721841)
XLA Ops:
  0.0 3.0 %collective-permute-start.2 = (bf16[8,4096]{1,0:T(8,128)(2,1)}, bf16[8,4096]{1,0:T(8,128)(2,1)S(1)}, u32[]{:S(2)}, u32[]{:S(2)}) collective-permute-start(bf16[8,4096]{1,0:T(8,128)(2,1)} %hidden_ref.1), channel_id=1, source_target_pairs={{0,24},{8,0},{16,8},{24,16},{1,25},{9,1},{17,9},{25,17},{2,26},{10... | collective-permute-start | bytes 196616 | tf_op jit(solution)/shard_map/ppermute | solution.py:26
  5.5 3.5 %collective-permute-done.1 = bf16[8,4096]{1,0:T(8,128)(2,1)S(1)} collective-permute-done((bf16[8,4096]{1,0:T(8,128)(2,1)}, bf16[8,4096]{1,0:T(8,128)(2,1)S(1)}, u32[]{:S(2)}, u32[]{:S(2)}) %collective-permute-start.1) | collective-permute-done | bytes 65568 | tf_op jit(solution)/shard_map/ppermute | solution.py:26
  10.6 2.0 collective-permute-start.3
  12.6 4.0 %collective-permute-start.4 = (bf16[32,4096]{1,0:T(8,128)(2,1)S(1)}, bf16[32,4096]{1,0:T(8,128)(2,1)S(1)}, u32[]{:S(2)}, u32[]{:S(2)}) collective-permute-start(bf16[32,4096]{1,0:T(8,128)(2,1)S(1)} %pad_maximum_fusion.2.refs_0_), channel_id=1, source_target_pairs={{0,224},{32,0},{64,32},{96,64},{128,96},{160,128},{192,160},{224,1... | collective-permute-start | bytes 786440 | tf_op jit(solution)/shard_map/ppermute | solution.py:26
  16.6 4.8 %collective-permute-done.3.refs_1_ = bf16[32,4096]{1,0:T(8,128)(2,1)S(1)} collective-permute-done((bf16[32,4096]{1,0:T(8,128)(2,1)S(1)}, bf16[32,4096]{1,0:T(8,128)(2,1)S(1)}, u32[]{:S(2)}, u32[]{:S(2)}) %collective-permute-start.3) | collective-permute-done | bytes 262176 | tf_op jit(solution)/shard_map/ppermute | solution.py:26
  21.4 3.2 %collective-permute-start.6 = (bf16[32,4096]{1,0:T(8,128)(2,1)S(1)}, bf16[32,4096]{1,0:T(8,128)(2,1)S(1)}, u32[]{:S(2)}, u32[]{:S(2)}) collective-permute-start(bf16[32,4096]{1,0:T(8,128)(2,1)S(1)} %collective-permute-done.4.refs_2_), channel_id=1, source_target_pairs={{0,224},{32,0},{64,32},{96,64},{128,96},{160,128},{192,160},{224,1... | collective-permute-start | bytes 786440 | tf_op jit(solution)/shard_map/ppermute | solution.py:26
  24.6 4.3 %collective-permute-done.5.refs_3_ = bf16[32,4096]{1,0:T(8,128)(2,1)S(1)} collective-permute-done((bf16[32,4096]{1,0:T(8,128)(2,1)S(1)}, bf16[32,4096]{1,0:T(8,128)(2,1)S(1)}, u32[]{:S(2)}, u32[]{:S(2)}) %collective-permute-start.5) | collective-permute-done | bytes 262176 | tf_op jit(solution)/shard_map/ppermute | solution.py:26
  30.4 3.2 %collective-permute-start.8 = (bf16[32,4096]{1,0:T(8,128)(2,1)S(1)}, bf16[32,4096]{1,0:T(8,128)(2,1)S(1)}, u32[]{:S(2)}, u32[]{:S(2)}) collective-permute-start(bf16[32,4096]{1,0:T(8,128)(2,1)S(1)} %collective-permute-done.6.refs_4_), channel_id=1, source_target_pairs={{0,224},{32,0},{64,32},{96,64},{128,96},{160,128},{192,160},{224,1... | collective-permute-start | bytes 786440 | tf_op jit(solution)/shard_map/ppermute | solution.py:26
  33.6 3.6 %collective-permute-done.7.refs_0_ = bf16[32,4096]{1,0:T(8,128)(2,1)S(1)} collective-permute-done((bf16[32,4096]{1,0:T(8,128)(2,1)S(1)}, bf16[32,4096]{1,0:T(8,128)(2,1)S(1)}, u32[]{:S(2)}, u32[]{:S(2)}) %collective-permute-start.7) | collective-permute-done | bytes 262176 | tf_op jit(solution)/shard_map/ppermute | solution.py:26
  39.1 2.4 collective-permute-start.18
  43.4 1.9 copy-done
  46.0 2.4 shard_map.91.first_ref
  48.5 2.2 shard_map.92
  50.7 1.9 all_gather.3.refs_0_
  52.9 1.8 collective-permute-start.10
  54.7 14.6 %collective-permute-done.11.refs_1_ = bf16[512,128]{1,0:T(8,128)(2,1)S(1)} collective-permute-done((bf16[512,128]{1,0:T(8,128)(2,1)S(1)}, bf16[512,128]{1,0:T(8,128)(2,1)S(1)}, u32[]{:S(2)}, u32[]{:S(2)}) %collective-permute-start.11) | collective-permute-done | bytes 131104 | tf_op jit(solution)/shard_map/ppermute | solution.py:26
  69.3 3.3 %collective-permute-start.14 = (bf16[512,128]{1,0:T(8,128)(2,1)S(1)}, bf16[512,128]{1,0:T(8,128)(2,1)S(1)}, u32[]{:S(2)}, u32[]{:S(2)}) collective-permute-start(bf16[512,128]{1,0:T(8,128)(2,1)S(1)} %all_gather.3.refs_0_), channel_id=1, source_target_pairs={{0,4},{2,6},{4,0},{6,2},{1,5},{3,7},{5,1},{7,3},{8,12},{10,14},{12... | collective-permute-start | bytes 393224 | tf_op jit(solution)/shard_map/ppermute | solution.py:26
  72.6 4.5 %shard_map.94 = (bf16[144,512]{1,0:T(8,128)(2,1)S(1)}, bf16[144,512]{1,0:T(8,128)(2,1)S(1)}) custom-call(s32[8,8]{1,0:T(8,128)S(1)} %stack.41.table_ref, bf16[256,128]{1,0:T(8,128)(2,1)S(1)} %get-tuple-element.36.k_ref, bf16[256,128]{1,0:T(8,128)(2,1)S(1)} %get-tuple-element.37.v_ref, bf16[2,1024,256]{2,1,0:T(8,128)(2,1)S(1)} %bitcast.17, ...), custom_call_target="tpu_custom_call" | custom-call | flops 671088640 | tf_op jit(solution)/shard_map/pallas_call | solution.py:38
  77.2 2.7 collective-permute-start.12
  79.9 2.6 shard_map.95
  83.1 2.8 collective-permute-start.15
  85.9 2.6 shard_map.93.refs_0_
  95.0 2.6 collective-permute-start.21
  97.7 2.6 collective-permute-start.20
  100.2 3.3 %all-to-all-start = ((bf16[4,64,128]{2,1,0:T(8,128)(2,1)}), bf16[4,64,128]{2,1,0:T(8,128)(2,1)S(1)}, u32[]{:S(2)}, u32[]{:S(2)}) async-start(bf16[4,64,128]{2,1,0:T(8,128)(2,1)} %shard_map.97), calls=%async_computation | async-start | bytes 131072 | tf_op jit(solution)/shard_map/all_to_all | solution.py:377
  103.6 41.4 %collective-permute-done.22.refs_3_ = bf16[128,4096]{1,0:T(8,128)(2,1)} collective-permute-done((bf16[128,4096]{1,0:T(8,128)(2,1)}, bf16[128,4096]{1,0:T(8,128)(2,1)}, u32[]{:S(2)}, u32[]{:S(2)}) %collective-permute-start.22) | collective-permute-done | bytes 1048608 | tf_op jit(solution)/shard_map/ppermute | solution.py:26
  145.5 3.4 %shard_map.98 = bf16[8,8,4096]{2,1,0:T(8,128)(2,1)S(1)} custom-call(s32[8,8]{1,0:T(8,128)S(1)} %stack.41.table_ref, bf16[4,64,128]{2,1,0:T(8,128)(2,1)S(1)} %all-to-all-done.heads_ref, bf16[128,4096]{1,0:T(8,128)(2,1)} %refs_0_, bf16[128,4096]{1,0:T(8,128)(2,1)} %collective-permute-done.20.refs_1_, bf16[128,4096]{1,0:T(8,128)(2,1)} %collective-permute-done.21.refs_2_, ...), custom_call_target="tpu_custom_call" | custom-call | tf_op jit(solution)/shard_map/pallas_call | solution.py:38
  148.9 22.2 %all_to_all.15.terms_ref = bf16[8,8,4096]{2,1,0:T(8,128)(2,1)S(1)} all-to-all(bf16[8,8,4096]{2,1,0:T(8,128)(2,1)S(1)} %shard_map.98), channel_id=1, replica_groups=mesh['z'=8,'y'=4,'x'=4,'c'=2] {'z'}, dimensions={0} | all-to-all | bytes 1048576 | tf_op jit(solution)/shard_map/all_to_all | solution.py:377
  171.9 3.6 %collective-permute-start.26 = (bf16[8,4096]{1,0:T(8,128)(2,1)S(1)}, bf16[8,4096]{1,0:T(8,128)(2,1)S(1)}, u32[]{:S(2)}, u32[]{:S(2)}) collective-permute-start(bf16[8,4096]{1,0:T(8,128)(2,1)S(1)} %get-tuple-element.54), channel_id=1, source_target_pairs={{0,24},{8,0},{16,8},{24,16},{1,25},{9,1},{17,9},{25,17},{2,26},{10... | collective-permute-start | bytes 196616 | tf_op jit(solution)/shard_map/ppermute | solution.py:26
  178.0 3.3 %collective-permute-done.25 = bf16[8,4096]{1,0:T(8,128)(2,1)S(1)} collective-permute-done((bf16[8,4096]{1,0:T(8,128)(2,1)S(1)}, bf16[8,4096]{1,0:T(8,128)(2,1)S(1)}, u32[]{:S(2)}, u32[]{:S(2)}) %collective-permute-start.25) | collective-permute-done | bytes 65568 | tf_op jit(solution)/shard_map/ppermute | solution.py:26
  182.6 7.7 %collective-permute-done.27.refs_1_ = bf16[32,4096]{1,0:T(8,128)(2,1)S(1)} collective-permute-done((bf16[32,4096]{1,0:T(8,128)(2,1)S(1)}, bf16[32,4096]{1,0:T(8,128)(2,1)S(1)}, u32[]{:S(2)}, u32[]{:S(2)}) %collective-permute-start.27) | collective-permute-done | bytes 262176 | tf_op jit(solution)/shard_map/ppermute | solution.py:26
  190.4 2.5 collective-permute-start.34
  193.3 2.5 collective-permute-start.32
  195.8 4.0 %collective-permute-done.29.refs_3_ = bf16[32,4096]{1,0:T(8,128)(2,1)S(1)} collective-permute-done((bf16[32,4096]{1,0:T(8,128)(2,1)S(1)}, bf16[32,4096]{1,0:T(8,128)(2,1)S(1)}, u32[]{:S(2)}, u32[]{:S(2)}) %collective-permute-start.29) | collective-permute-done | bytes 262176 | tf_op jit(solution)/shard_map/ppermute | solution.py:26
  200.1 3.8 %collective-permute-done.33 = bf16[344,512]{1,0:T(8,128)(2,1)S(1)} collective-permute-done((bf16[344,512]{1,0:T(8,128)(2,1)S(1)}, bf16[344,512]{1,0:T(8,128)(2,1)S(1)}, u32[]{:S(2)}, u32[]{:S(2)}) %collective-permute-start.33) | collective-permute-done | bytes 352288 | tf_op jit(solution)/shard_map/ppermute | solution.py:26
  204.8 2.6 collective-permute-done.31.refs_5_
  208.1 8.2 %collective-permute-done.28.refs_2_ = bf16[32,4096]{1,0:T(8,128)(2,1)S(1)} collective-permute-done((bf16[32,4096]{1,0:T(8,128)(2,1)S(1)}, bf16[32,4096]{1,0:T(8,128)(2,1)S(1)}, u32[]{:S(2)}, u32[]{:S(2)}) %collective-permute-start.28) | collective-permute-done | bytes 262176 | tf_op jit(solution)/shard_map/ppermute | solution.py:26
  218.0 6.2 %collective-permute-done.30.refs_4_ = bf16[32,4096]{1,0:T(8,128)(2,1)S(1)} collective-permute-done((bf16[32,4096]{1,0:T(8,128)(2,1)S(1)}, bf16[32,4096]{1,0:T(8,128)(2,1)S(1)}, u32[]{:S(2)}, u32[]{:S(2)}) %collective-permute-start.30) | collective-permute-done | bytes 262176 | tf_op jit(solution)/shard_map/ppermute | solution.py:26
  224.1 2.8 collective-permute-start.35
  227.0 4.4 %collective-permute-done.35.refs_6_ = bf16[32,4096]{1,0:T(8,128)(2,1)S(1)} collective-permute-done((bf16[32,4096]{1,0:T(8,128)(2,1)S(1)}, bf16[32,4096]{1,0:T(8,128)(2,1)S(1)}, u32[]{:S(2)}, u32[]{:S(2)}) %collective-permute-start.35) | collective-permute-done | bytes 262176 | tf_op jit(solution)/shard_map/ppermute | solution.py:26
  231.4 3.4 %collective-permute-done.36.refs_7_ = bf16[32,4096]{1,0:T(8,128)(2,1)S(1)} collective-permute-done((bf16[32,4096]{1,0:T(8,128)(2,1)S(1)}, bf16[32,4096]{1,0:T(8,128)(2,1)S(1)}, u32[]{:S(2)}, u32[]{:S(2)}) %collective-permute-start.36) | collective-permute-done | bytes 262176 | tf_op jit(solution)/shard_map/ppermute | solution.py:26
  234.8 5.1 %shard_map.100.x_ref = bf16[256,344]{1,0:T(8,128)(2,1)S(1)} custom-call(s32[8,8]{1,0:T(8,128)S(1)} %stack.41.table_ref, bf16[4,2,344,512]{3,2,1,0:T(8,128)(2,1)S(1)} %pad_maximum_fusion.near_ref, bf16[4,2,344,512]{3,2,1,0:T(8,128)(2,1)} %collective-permute-done.23.far_ref, bf16[32,4096]{1,0:T(8,128)(2,1)S(1)} %pad_maximum_fusion.3.refs_0_, ...), custom_call_target="tpu_custom_call" | custom-call | flops 1442840576 | tf_op jit(solution)/shard_map/pallas_call | solution.py:38
  240.0 3.0 %shard_map.101 = (bf16[64,4096]{1,0:T(8,128)(2,1)S(1)}, bf16[64,4096]{1,0:T(8,128)(2,1)S(1)}, bf16[64,4096]{1,0:T(8,128)(2,1)S(1)}, bf16[64,4096]{1,0:T(8,128)(2,1)S(1)}) custom-call(s32[8,8]{1,0:T(8,128)S(1)} %stack.41.table_ref, bf16[256,344]{1,0:T(8,128)(2,1)S(1)} %shard_map.100.x_ref, bf16[4,344,512]{2,1,0:T(8,128)(2,1)S(1)} %pad_maximum_fusion.1.refs_0_, ...), custom_call_target="tpu_custom_call" | custom-call | tf_op jit(solution)/shard_map/pallas_call | solution.py:38
  243.6 1.8 collective-permute-start.39
  246.8 11.1 %collective-permute-done.38.refs_1_ = bf16[64,4096]{1,0:T(8,128)(2,1)S(1)} collective-permute-done((bf16[64,4096]{1,0:T(8,128)(2,1)S(1)}, bf16[64,4096]{1,0:T(8,128)(2,1)S(1)}, u32[]{:S(2)}, u32[]{:S(2)}) %collective-permute-start.38) | collective-permute-done | bytes 524320 | tf_op jit(solution)/shard_map/ppermute | solution.py:26
  257.8 2.1 collective-permute-done.39.refs_2_
  259.9 7.6 %collective-permute-done.40.refs_3_ = bf16[64,4096]{1,0:T(8,128)(2,1)S(1)} collective-permute-done((bf16[64,4096]{1,0:T(8,128)(2,1)S(1)}, bf16[64,4096]{1,0:T(8,128)(2,1)S(1)}, u32[]{:S(2)}, u32[]{:S(2)}) %collective-permute-start.40) | collective-permute-done | bytes 524320 | tf_op jit(solution)/shard_map/ppermute | solution.py:26
  268.3 20.6 %all_to_all.16 = bf16[8,8,4096]{2,1,0:T(8,128)(2,1)S(1)} all-to-all(bf16[8,8,4096]{2,1,0:T(8,128)(2,1)S(1)} %shard_map.102), channel_id=1, replica_groups=mesh['z'=8,'y'=4,'x'=4,'c'=2] {'z'}, dimensions={0} | all-to-all | bytes 1048576 | tf_op jit(solution)/shard_map/all_to_all | solution.py:377
  (78 shorter events, 30.1 us)
Async XLA Ops:
  0.0 5.5 %collective-permute-start.2 = (bf16[8,4096]{1,0:T(8,128)(2,1)}, bf16[8,4096]{1,0:T(8,128)(2,1)S(1)}, u32[]{:S(2)}, u32[]{:S(2)}) collective-permute-start(bf16[8,4096]{1,0:T(8,128)(2,1)} %hidden_ref.1), channel_id=1, source_target_pairs={{0,24},{8,0},{16,8},{24,16},{1,25},{9,1},{17,9},{25,17},{2,26},{10... | collective-permute-start | bytes 196616 | tf_op jit(solution)/shard_map/ppermute | solution.py:26
  3.0 6.0 %collective-permute-start.1 = (bf16[8,4096]{1,0:T(8,128)(2,1)}, bf16[8,4096]{1,0:T(8,128)(2,1)S(1)}, u32[]{:S(2)}, u32[]{:S(2)}) collective-permute-start(bf16[8,4096]{1,0:T(8,128)(2,1)} %hidden_ref.1), channel_id=1, source_target_pairs={{0,16},{8,24},{16,0},{24,8},{1,17},{9,25},{17,1},{25,9},{2,18},{10... | collective-permute-start | bytes 196616 | tf_op jit(solution)/shard_map/ppermute | solution.py:26
  3.6 6.1 %collective-permute-start = (bf16[8,4096]{1,0:T(8,128)(2,1)}, bf16[8,4096]{1,0:T(8,128)(2,1)S(1)}, u32[]{:S(2)}, u32[]{:S(2)}) collective-permute-start(bf16[8,4096]{1,0:T(8,128)(2,1)} %hidden_ref.1), channel_id=1, source_target_pairs={{0,8},{8,16},{16,24},{24,0},{1,9},{9,17},{17,25},{25,1},{2,10},{10... | collective-permute-start | bytes 196616 | tf_op jit(solution)/shard_map/ppermute | solution.py:26
  10.6 10.8 %collective-permute-start.3 = (bf16[32,4096]{1,0:T(8,128)(2,1)S(1)}, bf16[32,4096]{1,0:T(8,128)(2,1)S(1)}, u32[]{:S(2)}, u32[]{:S(2)}) collective-permute-start(bf16[32,4096]{1,0:T(8,128)(2,1)S(1)} %pad_maximum_fusion.2.refs_0_), channel_id=1, source_target_pairs={{0,32},{32,64},{64,96},{96,128},{128,160},{160,192},{192,224},{224... | collective-permute-start | bytes 786440 | tf_op jit(solution)/shard_map/ppermute | solution.py:26
  12.6 8.8 %collective-permute-start.4 = (bf16[32,4096]{1,0:T(8,128)(2,1)S(1)}, bf16[32,4096]{1,0:T(8,128)(2,1)S(1)}, u32[]{:S(2)}, u32[]{:S(2)}) collective-permute-start(bf16[32,4096]{1,0:T(8,128)(2,1)S(1)} %pad_maximum_fusion.2.refs_0_), channel_id=1, source_target_pairs={{0,224},{32,0},{64,32},{96,64},{128,96},{160,128},{192,160},{224,1... | collective-permute-start | bytes 786440 | tf_op jit(solution)/shard_map/ppermute | solution.py:26
  21.4 7.6 %collective-permute-start.5 = (bf16[32,4096]{1,0:T(8,128)(2,1)S(1)}, bf16[32,4096]{1,0:T(8,128)(2,1)S(1)}, u32[]{:S(2)}, u32[]{:S(2)}) collective-permute-start(bf16[32,4096]{1,0:T(8,128)(2,1)S(1)} %collective-permute-done.3.refs_1_), channel_id=1, source_target_pairs={{0,32},{32,64},{64,96},{96,128},{128,160},{160,192},{192,224},{224... | collective-permute-start | bytes 786440 | tf_op jit(solution)/shard_map/ppermute | solution.py:26
  21.4 9.0 %collective-permute-start.6 = (bf16[32,4096]{1,0:T(8,128)(2,1)S(1)}, bf16[32,4096]{1,0:T(8,128)(2,1)S(1)}, u32[]{:S(2)}, u32[]{:S(2)}) collective-permute-start(bf16[32,4096]{1,0:T(8,128)(2,1)S(1)} %collective-permute-done.4.refs_2_), channel_id=1, source_target_pairs={{0,224},{32,0},{64,32},{96,64},{128,96},{160,128},{192,160},{224,1... | collective-permute-start | bytes 786440 | tf_op jit(solution)/shard_map/ppermute | solution.py:26
  29.0 8.2 %collective-permute-start.7 = (bf16[32,4096]{1,0:T(8,128)(2,1)S(1)}, bf16[32,4096]{1,0:T(8,128)(2,1)S(1)}, u32[]{:S(2)}, u32[]{:S(2)}) collective-permute-start(bf16[32,4096]{1,0:T(8,128)(2,1)S(1)} %collective-permute-done.5.refs_3_), channel_id=1, source_target_pairs={{0,32},{32,64},{64,96},{96,128},{128,160},{160,192},{192,224},{224... | collective-permute-start | bytes 786440 | tf_op jit(solution)/shard_map/ppermute | solution.py:26
  30.4 18.2 %collective-permute-start.8 = (bf16[32,4096]{1,0:T(8,128)(2,1)S(1)}, bf16[32,4096]{1,0:T(8,128)(2,1)S(1)}, u32[]{:S(2)}, u32[]{:S(2)}) collective-permute-start(bf16[32,4096]{1,0:T(8,128)(2,1)S(1)} %collective-permute-done.6.refs_4_), channel_id=1, source_target_pairs={{0,224},{32,0},{64,32},{96,64},{128,96},{160,128},{192,160},{224,1... | collective-permute-start | bytes 786440 | tf_op jit(solution)/shard_map/ppermute | solution.py:26
  37.2 11.3 %collective-permute-start.9 = (bf16[32,4096]{1,0:T(8,128)(2,1)S(1)}, bf16[32,4096]{1,0:T(8,128)(2,1)S(1)}, u32[]{:S(2)}, u32[]{:S(2)}) collective-permute-start(bf16[32,4096]{1,0:T(8,128)(2,1)S(1)} %collective-permute-done.7.refs_0_), channel_id=1, source_target_pairs={{0,32},{32,64},{64,96},{96,128},{128,160},{160,192},{192,224},{224... | collective-permute-start | bytes 786440 | tf_op jit(solution)/shard_map/ppermute | solution.py:26
  38.5 54.7 %collective-permute-start.19 = (bf16[2,344,512]{2,1,0:T(8,128)(2,1)}, bf16[2,344,512]{2,1,0:T(8,128)(2,1)S(1)}, u32[]{:S(2)}, u32[]{:S(2)}) collective-permute-start(bf16[2,344,512]{2,1,0:T(8,128)(2,1)} %bitcast.23), channel_id=1, source_target_pairs={{0,6},{2,0},{4,2},{6,4},{1,7},{3,1},{5,3},{7,5},{8,14},{10,8},{12,... | collective-permute-start | bytes 2113544 | tf_op jit(solution)/shard_map/ppermute | solution.py:26
  39.1 54.1 %collective-permute-start.18 = (bf16[2,344,512]{2,1,0:T(8,128)(2,1)}, bf16[2,344,512]{2,1,0:T(8,128)(2,1)}, u32[]{:S(2)}, u32[]{:S(2)}) collective-permute-start(bf16[2,344,512]{2,1,0:T(8,128)(2,1)} %bitcast.24), channel_id=1, source_target_pairs={{0,4},{2,6},{4,0},{6,2},{1,5},{3,7},{5,1},{7,3},{8,12},{10,14},{12... | collective-permute-start | bytes 2113544 | tf_op jit(solution)/shard_map/ppermute | solution.py:26
  41.6 51.7 %collective-permute-start.17 = (bf16[2,344,512]{2,1,0:T(8,128)(2,1)}, bf16[2,344,512]{2,1,0:T(8,128)(2,1)}, u32[]{:S(2)}, u32[]{:S(2)}) collective-permute-start(bf16[2,344,512]{2,1,0:T(8,128)(2,1)} %bitcast.25), channel_id=1, source_target_pairs={{0,2},{2,4},{4,6},{6,0},{1,3},{3,5},{5,7},{7,1},{8,10},{10,12},{12... | collective-permute-start | bytes 2113544 | tf_op jit(solution)/shard_map/ppermute | solution.py:26
  43.4 1.9 copy-start
  48.5 24.1 %copy-start.1 = (bf16[2,1024,1,256]{3,1,2,0:T(8,128)(2,1)S(1)}, bf16[2,1024,1,256]{3,1,2,0:T(8,128)(2,1)}, u32[]{:S(2)}) copy-start(bf16[2,1024,1,256]{3,1,2,0:T(8,128)(2,1)} %param.12) | copy-start | bytes 3145732
  52.6 16.6 %collective-permute-start.11 = (bf16[512,128]{1,0:T(8,128)(2,1)S(1)}, bf16[512,128]{1,0:T(8,128)(2,1)S(1)}, u32[]{:S(2)}, u32[]{:S(2)}) collective-permute-start(bf16[512,128]{1,0:T(8,128)(2,1)S(1)} %all_gather.3.refs_0_), channel_id=1, source_target_pairs={{0,6},{2,0},{4,2},{6,4},{1,7},{3,1},{5,3},{7,5},{8,14},{10,8},{12,... | collective-permute-start | bytes 393224 | tf_op jit(solution)/shard_map/ppermute | solution.py:26
  52.9 19.8 %collective-permute-start.10 = (bf16[512,128]{1,0:T(8,128)(2,1)S(1)}, bf16[512,128]{1,0:T(8,128)(2,1)S(1)}, u32[]{:S(2)}, u32[]{:S(2)}) collective-permute-start(bf16[512,128]{1,0:T(8,128)(2,1)S(1)} %all_gather.3.refs_0_), channel_id=1, source_target_pairs={{0,2},{2,4},{4,6},{6,0},{1,3},{3,5},{5,7},{7,1},{8,10},{10,12},{12... | collective-permute-start | bytes 393224 | tf_op jit(solution)/shard_map/ppermute | solution.py:26
  69.3 10.6 %collective-permute-start.14 = (bf16[512,128]{1,0:T(8,128)(2,1)S(1)}, bf16[512,128]{1,0:T(8,128)(2,1)S(1)}, u32[]{:S(2)}, u32[]{:S(2)}) collective-permute-start(bf16[512,128]{1,0:T(8,128)(2,1)S(1)} %all_gather.3.refs_0_), channel_id=1, source_target_pairs={{0,4},{2,6},{4,0},{6,2},{1,5},{3,7},{5,1},{7,3},{8,12},{10,14},{12... | collective-permute-start | bytes 393224 | tf_op jit(solution)/shard_map/ppermute | solution.py:26
  72.6 20.6 %copy-start.5 = (bf16[512,2,344]{0,2,1:T(8,128)(2,1)S(1)}, bf16[512,2,344]{0,2,1:T(8,128)(2,1)}, u32[]{:S(2)}) copy-start(bf16[512,2,344]{0,2,1:T(8,128)(2,1)} %param.16) | copy-start | bytes 2113540
  77.2 6.0 %collective-permute-start.12 = (bf16[144,512]{1,0:T(8,128)(2,1)S(1)}, bf16[144,512]{1,0:T(8,128)(2,1)S(1)}, u32[]{:S(2)}, u32[]{:S(2)}) collective-permute-start(bf16[144,512]{1,0:T(8,128)(2,1)S(1)} %get-tuple-element.39), channel_id=1, source_target_pairs={{0,6},{2,0},{4,2},{6,4},{1,7},{3,1},{5,3},{7,5},{8,14},{10,8},{12,... | collective-permute-start | bytes 442376 | tf_op jit(solution)/shard_map/ppermute | solution.py:26
  79.9 8.7 %collective-permute-start.13 = (bf16[144,512]{1,0:T(8,128)(2,1)S(1)}, bf16[144,512]{1,0:T(8,128)(2,1)S(1)}, u32[]{:S(2)}, u32[]{:S(2)}) collective-permute-start(bf16[144,512]{1,0:T(8,128)(2,1)S(1)} %get-tuple-element.40), channel_id=1, source_target_pairs={{0,2},{2,4},{4,6},{6,0},{1,3},{3,5},{5,7},{7,1},{8,10},{10,12},{12... | collective-permute-start | bytes 442376 | tf_op jit(solution)/shard_map/ppermute | solution.py:26
  83.1 6.6 %collective-permute-start.15 = (bf16[144,512]{1,0:T(8,128)(2,1)S(1)}, bf16[144,512]{1,0:T(8,128)(2,1)S(1)}, u32[]{:S(2)}, u32[]{:S(2)}) collective-permute-start(bf16[144,512]{1,0:T(8,128)(2,1)S(1)} %shard_map.95), channel_id=1, source_target_pairs={{0,4},{2,6},{4,0},{6,2},{1,5},{3,7},{5,1},{7,3},{8,12},{10,14},{12... | collective-permute-start | bytes 442376 | tf_op jit(solution)/shard_map/ppermute | solution.py:26
  90.5 1.4 collective-permute-start.16
  94.8 77.1 %collective-permute-start.23 = (bf16[4,2,344,512]{3,2,1,0:T(8,128)(2,1)S(1)}, bf16[4,2,344,512]{3,2,1,0:T(8,128)(2,1)}, u32[]{:S(2)}, u32[]{:S(2)}) collective-permute-start(bf16[4,2,344,512]{3,2,1,0:T(8,128)(2,1)S(1)} %pad_maximum_fusion.near_ref), channel_id=1, source_target_pairs={{0,1},{1,0},{2,3},{3,2},{4,5},{5,4},{6,7},{7,6},{8,9},{9,8},{10,11... | collective-permute-start | bytes 8454152 | tf_op jit(solution)/shard_map/ppermute | solution.py:26
  95.0 49.9 %collective-permute-start.22 = (bf16[128,4096]{1,0:T(8,128)(2,1)}, bf16[128,4096]{1,0:T(8,128)(2,1)}, u32[]{:S(2)}, u32[]{:S(2)}) collective-permute-start(bf16[128,4096]{1,0:T(8,128)(2,1)} %refs_0_), channel_id=1, source_target_pairs={{0,8},{8,16},{16,24},{24,0},{1,9},{9,17},{17,25},{25,1},{2,10},{10... | collective-permute-start | bytes 3145736 | tf_op jit(solution)/shard_map/ppermute | solution.py:26
  95.0 49.9 %collective-permute-start.21 = (bf16[128,4096]{1,0:T(8,128)(2,1)}, bf16[128,4096]{1,0:T(8,128)(2,1)}, u32[]{:S(2)}, u32[]{:S(2)}) collective-permute-start(bf16[128,4096]{1,0:T(8,128)(2,1)} %refs_0_), channel_id=1, source_target_pairs={{0,16},{8,24},{16,0},{24,8},{1,17},{9,25},{17,1},{25,9},{2,18},{10... | collective-permute-start | bytes 3145736 | tf_op jit(solution)/shard_map/ppermute | solution.py:26
  97.7 47.8 %collective-permute-start.20 = (bf16[128,4096]{1,0:T(8,128)(2,1)}, bf16[128,4096]{1,0:T(8,128)(2,1)}, u32[]{:S(2)}, u32[]{:S(2)}) collective-permute-start(bf16[128,4096]{1,0:T(8,128)(2,1)} %refs_0_), channel_id=1, source_target_pairs={{0,24},{8,0},{16,8},{24,16},{1,25},{9,1},{17,9},{25,17},{2,26},{10... | collective-permute-start | bytes 3145736 | tf_op jit(solution)/shard_map/ppermute | solution.py:26
  100.2 45.3 %all-to-all-start = ((bf16[4,64,128]{2,1,0:T(8,128)(2,1)}), bf16[4,64,128]{2,1,0:T(8,128)(2,1)S(1)}, u32[]{:S(2)}, u32[]{:S(2)}) async-start(bf16[4,64,128]{2,1,0:T(8,128)(2,1)} %shard_map.97), calls=%async_computation | async-start | bytes 131072 | tf_op jit(solution)/shard_map/all_to_all | solution.py:377
  103.5 67.5 %copy-start.2 = (bf16[8,4096]{1,0:T(8,128)(2,1)S(1)}, bf16[8,4096]{1,0:T(8,128)(2,1)}, u32[]{:S(2)}) copy-start(bf16[8,4096]{1,0:T(8,128)(2,1)} %hidden_ref.1) | copy-start | bytes 196612
  103.5 67.5 %copy-start.4 = (f32[4096]{0:T(1024)S(1)}, f32[4096]{0:T(1024)}, u32[]{:S(2)}) copy-start(f32[4096]{0:T(1024)} %param.15) | copy-start | bytes 49156
  103.5 86.8 %copy-start.6 = (bf16[344,512]{1,0:T(8,128)(2,1)S(1)}, bf16[344,512]{1,0:T(8,128)(2,1)}, u32[]{:S(2)}) copy-start(bf16[344,512]{1,0:T(8,128)(2,1)} %param.17) | copy-start | bytes 1056772
  171.9 6.1 %collective-permute-start.26 = (bf16[8,4096]{1,0:T(8,128)(2,1)S(1)}, bf16[8,4096]{1,0:T(8,128)(2,1)S(1)}, u32[]{:S(2)}, u32[]{:S(2)}) collective-permute-start(bf16[8,4096]{1,0:T(8,128)(2,1)S(1)} %get-tuple-element.54), channel_id=1, source_target_pairs={{0,24},{8,0},{16,8},{24,16},{1,25},{9,1},{17,9},{25,17},{2,26},{10... | collective-permute-start | bytes 196616 | tf_op jit(solution)/shard_map/ppermute | solution.py:26
  175.5 5.8 %collective-permute-start.25 = (bf16[8,4096]{1,0:T(8,128)(2,1)S(1)}, bf16[8,4096]{1,0:T(8,128)(2,1)S(1)}, u32[]{:S(2)}, u32[]{:S(2)}) collective-permute-start(bf16[8,4096]{1,0:T(8,128)(2,1)S(1)} %get-tuple-element.54), channel_id=1, source_target_pairs={{0,16},{8,24},{16,0},{24,8},{1,17},{9,25},{17,1},{25,9},{2,18},{10... | collective-permute-start | bytes 196616 | tf_op jit(solution)/shard_map/ppermute | solution.py:26
  176.4 5.5 %collective-permute-start.24 = (bf16[8,4096]{1,0:T(8,128)(2,1)S(1)}, bf16[8,4096]{1,0:T(8,128)(2,1)S(1)}, u32[]{:S(2)}, u32[]{:S(2)}) collective-permute-start(bf16[8,4096]{1,0:T(8,128)(2,1)S(1)} %get-tuple-element.54), channel_id=1, source_target_pairs={{0,8},{8,16},{16,24},{24,0},{1,9},{9,17},{17,25},{25,1},{2,10},{10... | collective-permute-start | bytes 196616 | tf_op jit(solution)/shard_map/ppermute | solution.py:26
  182.0 8.4 %collective-permute-start.27 = (bf16[32,4096]{1,0:T(8,128)(2,1)S(1)}, bf16[32,4096]{1,0:T(8,128)(2,1)S(1)}, u32[]{:S(2)}, u32[]{:S(2)}) collective-permute-start(bf16[32,4096]{1,0:T(8,128)(2,1)S(1)} %pad_maximum_fusion.3.refs_0_), channel_id=1, source_target_pairs={{0,32},{32,64},{64,96},{96,128},{128,160},{160,192},{192,224},{224... | collective-permute-start | bytes 786440 | tf_op jit(solution)/shard_map/ppermute | solution.py:26
  190.3 9.5 %collective-permute-start.29 = (bf16[32,4096]{1,0:T(8,128)(2,1)S(1)}, bf16[32,4096]{1,0:T(8,128)(2,1)S(1)}, u32[]{:S(2)}, u32[]{:S(2)}) collective-permute-start(bf16[32,4096]{1,0:T(8,128)(2,1)S(1)} %collective-permute-done.27.refs_1_), channel_id=1, source_target_pairs={{0,32},{32,64},{64,96},{96,128},{128,160},{160,192},{192,224},{224... | collective-permute-start | bytes 786440 | tf_op jit(solution)/shard_map/ppermute | solution.py:26
  190.4 9.7 %collective-permute-start.34 = (bf16[344,512]{1,0:T(8,128)(2,1)S(1)}, bf16[344,512]{1,0:T(8,128)(2,1)S(1)}, u32[]{:S(2)}, u32[]{:S(2)}) collective-permute-start(bf16[344,512]{1,0:T(8,128)(2,1)S(1)} %copy-done.6), channel_id=1, source_target_pairs={{0,6},{2,0},{4,2},{6,4},{1,7},{3,1},{5,3},{7,5},{8,14},{10,8},{12,... | collective-permute-start | bytes 1056776 | tf_op jit(solution)/shard_map/ppermute | solution.py:26
  192.8 11.0 %collective-permute-start.33 = (bf16[344,512]{1,0:T(8,128)(2,1)S(1)}, bf16[344,512]{1,0:T(8,128)(2,1)S(1)}, u32[]{:S(2)}, u32[]{:S(2)}) collective-permute-start(bf16[344,512]{1,0:T(8,128)(2,1)S(1)} %copy-done.6), channel_id=1, source_target_pairs={{0,4},{2,6},{4,0},{6,2},{1,5},{3,7},{5,1},{7,3},{8,12},{10,14},{12... | collective-permute-start | bytes 1056776 | tf_op jit(solution)/shard_map/ppermute | solution.py:26
  193.3 11.6 %collective-permute-start.32 = (bf16[344,512]{1,0:T(8,128)(2,1)S(1)}, bf16[344,512]{1,0:T(8,128)(2,1)S(1)}, u32[]{:S(2)}, u32[]{:S(2)}) collective-permute-start(bf16[344,512]{1,0:T(8,128)(2,1)S(1)} %copy-done.6), channel_id=1, source_target_pairs={{0,2},{2,4},{4,6},{6,0},{1,3},{3,5},{5,7},{7,1},{8,10},{10,12},{12... | collective-permute-start | bytes 1056776 | tf_op jit(solution)/shard_map/ppermute | solution.py:26
  199.8 7.6 %collective-permute-start.31 = (bf16[32,4096]{1,0:T(8,128)(2,1)S(1)}, bf16[32,4096]{1,0:T(8,128)(2,1)S(1)}, u32[]{:S(2)}, u32[]{:S(2)}) collective-permute-start(bf16[32,4096]{1,0:T(8,128)(2,1)S(1)} %collective-permute-done.29.refs_3_), channel_id=1, source_target_pairs={{0,32},{32,64},{64,96},{96,128},{128,160},{160,192},{192,224},{224... | collective-permute-start | bytes 786440 | tf_op jit(solution)/shard_map/ppermute | solution.py:26
  207.6 32.4 %collective-permute-start.37 = (bf16[4,344,512]{2,1,0:T(8,128)(2,1)S(1)}, bf16[4,344,512]{2,1,0:T(8,128)(2,1)S(1)}, u32[]{:S(2)}, u32[]{:S(2)}) collective-permute-start(bf16[4,344,512]{2,1,0:T(8,128)(2,1)S(1)} %pad_maximum_fusion.1.refs_0_), channel_id=1, source_target_pairs={{0,1},{1,0},{2,3},{3,2},{4,5},{5,4},{6,7},{7,6},{8,9},{9,8},{10,11... | collective-permute-start | bytes 4227080 | tf_op jit(solution)/shard_map/ppermute | solution.py:26
  207.7 8.7 %collective-permute-start.28 = (bf16[32,4096]{1,0:T(8,128)(2,1)S(1)}, bf16[32,4096]{1,0:T(8,128)(2,1)S(1)}, u32[]{:S(2)}, u32[]{:S(2)}) collective-permute-start(bf16[32,4096]{1,0:T(8,128)(2,1)S(1)} %pad_maximum_fusion.3.refs_0_), channel_id=1, source_target_pairs={{0,224},{32,0},{64,32},{96,64},{128,96},{160,128},{192,160},{224,1... | collective-permute-start | bytes 786440 | tf_op jit(solution)/shard_map/ppermute | solution.py:26
  216.4 7.8 %collective-permute-start.30 = (bf16[32,4096]{1,0:T(8,128)(2,1)S(1)}, bf16[32,4096]{1,0:T(8,128)(2,1)S(1)}, u32[]{:S(2)}, u32[]{:S(2)}) collective-permute-start(bf16[32,4096]{1,0:T(8,128)(2,1)S(1)} %collective-permute-done.28.refs_2_), channel_id=1, source_target_pairs={{0,224},{32,0},{64,32},{96,64},{128,96},{160,128},{192,160},{224,1... | collective-permute-start | bytes 786440 | tf_op jit(solution)/shard_map/ppermute | solution.py:26
  224.1 7.3 %collective-permute-start.35 = (bf16[32,4096]{1,0:T(8,128)(2,1)S(1)}, bf16[32,4096]{1,0:T(8,128)(2,1)S(1)}, u32[]{:S(2)}, u32[]{:S(2)}) collective-permute-start(bf16[32,4096]{1,0:T(8,128)(2,1)S(1)} %collective-permute-done.30.refs_4_), channel_id=1, source_target_pairs={{0,224},{32,0},{64,32},{96,64},{128,96},{160,128},{192,160},{224,1... | collective-permute-start | bytes 786440 | tf_op jit(solution)/shard_map/ppermute | solution.py:26
  227.0 7.8 %collective-permute-start.36 = (bf16[32,4096]{1,0:T(8,128)(2,1)S(1)}, bf16[32,4096]{1,0:T(8,128)(2,1)S(1)}, u32[]{:S(2)}, u32[]{:S(2)}) collective-permute-start(bf16[32,4096]{1,0:T(8,128)(2,1)S(1)} %collective-permute-done.31.refs_5_), channel_id=1, source_target_pairs={{0,32},{32,64},{64,96},{96,128},{128,160},{160,192},{192,224},{224... | collective-permute-start | bytes 786440 | tf_op jit(solution)/shard_map/ppermute | solution.py:26
  242.9 14.9 %collective-permute-start.38 = (bf16[64,4096]{1,0:T(8,128)(2,1)S(1)}, bf16[64,4096]{1,0:T(8,128)(2,1)S(1)}, u32[]{:S(2)}, u32[]{:S(2)}) collective-permute-start(bf16[64,4096]{1,0:T(8,128)(2,1)S(1)} %get-tuple-element.62), channel_id=1, source_target_pairs={{0,24},{8,0},{16,8},{24,16},{1,25},{9,1},{17,9},{25,17},{2,26},{10... | collective-permute-start | bytes 1572872 | tf_op jit(solution)/shard_map/ppermute | solution.py:26
  243.6 16.3 %collective-permute-start.39 = (bf16[64,4096]{1,0:T(8,128)(2,1)S(1)}, bf16[64,4096]{1,0:T(8,128)(2,1)S(1)}, u32[]{:S(2)}, u32[]{:S(2)}) collective-permute-start(bf16[64,4096]{1,0:T(8,128)(2,1)S(1)} %get-tuple-element.63), channel_id=1, source_target_pairs={{0,16},{8,24},{16,0},{24,8},{1,17},{9,25},{17,1},{25,9},{2,18},{10... | collective-permute-start | bytes 1572872 | tf_op jit(solution)/shard_map/ppermute | solution.py:26
  245.4 22.0 %collective-permute-start.40 = (bf16[64,4096]{1,0:T(8,128)(2,1)S(1)}, bf16[64,4096]{1,0:T(8,128)(2,1)S(1)}, u32[]{:S(2)}, u32[]{:S(2)}) collective-permute-start(bf16[64,4096]{1,0:T(8,128)(2,1)S(1)} %get-tuple-element.64), channel_id=1, source_target_pairs={{0,8},{8,16},{16,24},{24,0},{1,9},{9,17},{17,25},{25,1},{2,10},{10... | collective-permute-start | bytes 1572872 | tf_op jit(solution)/shard_map/ppermute | solution.py:26
  (1 other events, 0.7 us)
where the time goes:
time: 292 us; the launch traced here: 290 us
  waiting for transfers between devices  145 us (50%)
  starting transfers between devices  61.1 us (21%)
  blocking collectives  44.6 us (15%)
  Pallas kernels  29.7 us (10%)
  other arithmetic  4.63 us (2%)
  local copies, waits for them, and re-layouts  4.04 us (1%)
    ppermute x41, waiting for transfers between devices, shifted(): lax.ppermute(value, axis, [(i, (i + step) % count) for i in range(count)])  145 us
    ppermute x41, starting transfers between devices, shifted(): lax.ppermute(value, axis, [(i, (i + step) % count) for i in range(count)])  57.8 us
    all_to_all x2, blocking collectives, exchanged(): return lax.all_to_all(value, axis, split_axis=0, concat_axis=0, tiled=True)  42.7 us
    pallas_call x12, Pallas kernels, run(): pl.pallas_call(kernel, in_specs=[pl.BlockSpec(memory_space=pltpu.SMEM)] +...  29.7 us
  transfers between devices with their start and end apart: 42, of which 29 were waited for; matrix products, arithmetic and copies ran while one was open for 1% of the time, Pallas kernels for 9%

commit v1 on v0

--- a/solution.py
+++ b/solution.py
@@ -333,7 +333,10 @@
     side, _, width = weights[0].shape
     shape = (rows.shape[0] // lanes, side * width * len(weights))
     return run(
-        functools.partial(down_kernel, lanes), table, [rows, *weights], [(shape, BF16)] * lanes
+        functools.partial(down_kernel, lanes),
+        table,
+        [rows, *weights],
+        [(shape, BF16)] * lanes,
     )
 
 
@@ -377,9 +380,9 @@
         return lax.all_to_all(value, axis, split_axis=0, concat_axis=0, tiled=True)
 
     r0 = gather_y(hidden_in)
-    r0, w_gate_up, w_out, w_down = tied((r0, w_gate_up.transpose(1, 2, 0), w_out, w_down))
+    r0, w_out, w_down = tied((r0, w_out, w_down))
     f1, b1 = shifted(r0, "z", 1), shifted(r0, "z", -1)
-    gates = gathered_turned(w_gate_up, "x")
+    gates = gathered_turned(w_gate_up.transpose(1, 2, 0), "x")
     f2, b2 = shifted(f1, "z", 1), shifted(b1, "z", -1)
     w_heads = along_y(w_out)
     f3, b3 = shifted(f2, "z", 1), shifted(b2, "z", -1)
@@ -411,7 +414,6 @@
     f1, b1 = shifted(r0, "z", 1), shifted(r0, "z", -1)
     f2, b2 = shifted(f1, "z", 1), shifted(b1, "z", -1)
     f3, b3 = shifted(f2, "z", 1), shifted(b2, "z", -1)
-    f3, downs = tied((f3, downs))
     downs = jnp.stack(downs)
     downs = [downs, shifted(downs, "c", 1)]
     f4 = shifted(f3, "z", 1)

time: 292 us -> 257 us (0.88)
  waiting for transfers between devices: 145 us -> 122 us
  blocking collectives: 44.6 us -> 25.2 us
  starting transfers between devices: 61.1 us -> 65.7 us
    ppermute x41, waiting for transfers between devices: 145 us -> 109 us  [shifted(): lax.ppermute(value, axis, [(i, (i + step) % count) for i in range(count)])]
    all_to_all x2 -> x1, blocking collectives: 42.7 us -> 23.3 us  [exchanged(): return lax.all_to_all(value, axis, split_axis=0, concat_axis=0, tiled=True)]
    all_to_all x1 -> x2, waiting for transfers between devices: 0.07 us -> 12.9 us  [exchanged(): return lax.all_to_all(value, axis, split_axis=0, concat_axis=0, tiled=True)]
    all_to_all x1 -> x2, starting transfers between devices: 3.28 us -> 9.47 us  [exchanged(): return lax.all_to_all(value, axis, split_axis=0, concat_axis=0, tiled=True)]
  transfers between devices with their start and end apart: 42 -> 43, of which waited for: 29 -> 26; matrix products, arithmetic and copies ran while one was open for 1% -> 2% of each run, Pallas kernels for 9% -> 10%
where the time goes in v1:
time: 257 us; the launch traced here: 255 us
  waiting for transfers between devices  122 us (47%)
  starting transfers between devices  65.7 us (26%)
  Pallas kernels  29.6 us (12%)
  blocking collectives  25.2 us (10%)
  other arithmetic  5.9 us (2%)
  local copies, waits for them, and re-layouts  5.66 us (2%)
    ppermute x41, waiting for transfers between devices, shifted(): lax.ppermute(value, axis, [(i, (i + step) % count) for i in range(count)])  109 us
    ppermute x41, starting transfers between devices, shifted(): lax.ppermute(value, axis, [(i, (i + step) % count) for i in range(count)])  56.3 us
    pallas_call x12, Pallas kernels, run(): pl.pallas_call(kernel, in_specs=[pl.BlockSpec(memory_space=pltpu.SMEM)] +...  29.6 us
    all_to_all x1, blocking collectives, exchanged(): return lax.all_to_all(value, axis, split_axis=0, concat_axis=0, tiled=True)  23.3 us
    all_to_all x2, waiting for transfers between devices, exchanged(): return lax.all_to_all(value, axis, split_axis=0, concat_axis=0, tiled=True)  12.9 us
    all_to_all x2, starting transfers between devices, exchanged(): return lax.all_to_all(value, axis, split_axis=0, concat_axis=0, tiled=True)  9.47 us
  transfers between devices with their start and end apart: 43, of which 26 were waited for; matrix products, arithmetic and copies ran while one was open for 2% of the time, Pallas kernels for 10%

profile of v1, /device:TPU:2, one launch (start us, length us, event | category | flops | bytes accessed | tf_op | source)
XLA Modules:
  0.0 254.7 jit_solution(13073001939425248089)
XLA Ops:
  0.0 3.0 %collective-permute-start.2 = (bf16[8,4096]{1,0:T(8,128)(2,1)}, bf16[8,4096]{1,0:T(8,128)(2,1)S(1)}, u32[]{:S(2)}, u32[]{:S(2)}) collective-permute-start(bf16[8,4096]{1,0:T(8,128)(2,1)} %hidden_ref.1), channel_id=1, source_target_pairs={{0,24},{8,0},{16,8},{24,16},{1,25},{9,1},{17,9},{25,17},{2,26},{10... | collective-permute-start | bytes 196616 | tf_op jit(solution)/shard_map/ppermute | solution.py:26
  5.5 3.5 %collective-permute-done.1 = bf16[8,4096]{1,0:T(8,128)(2,1)S(1)} collective-permute-done((bf16[8,4096]{1,0:T(8,128)(2,1)}, bf16[8,4096]{1,0:T(8,128)(2,1)S(1)}, u32[]{:S(2)}, u32[]{:S(2)}) %collective-permute-start.1) | collective-permute-done | bytes 65568 | tf_op jit(solution)/shard_map/ppermute | solution.py:26
  10.6 2.0 collective-permute-start.3
  12.6 4.0 %collective-permute-start.4 = (bf16[32,4096]{1,0:T(8,128)(2,1)S(1)}, bf16[32,4096]{1,0:T(8,128)(2,1)S(1)}, u32[]{:S(2)}, u32[]{:S(2)}) collective-permute-start(bf16[32,4096]{1,0:T(8,128)(2,1)S(1)} %pad_maximum_fusion.2.refs_0_), channel_id=1, source_target_pairs={{0,224},{32,0},{64,32},{96,64},{128,96},{160,128},{192,160},{224,1... | collective-permute-start | bytes 786440 | tf_op jit(solution)/shard_map/ppermute | solution.py:26
  16.6 4.8 %collective-permute-done.3.refs_1_ = bf16[32,4096]{1,0:T(8,128)(2,1)S(1)} collective-permute-done((bf16[32,4096]{1,0:T(8,128)(2,1)S(1)}, bf16[32,4096]{1,0:T(8,128)(2,1)S(1)}, u32[]{:S(2)}, u32[]{:S(2)}) %collective-permute-start.3) | collective-permute-done | bytes 262176 | tf_op jit(solution)/shard_map/ppermute | solution.py:26
  21.4 1.5 collective-permute-start.17
  24.0 2.2 collective-permute-start.19
  26.1 3.2 %collective-permute-start.6 = (bf16[32,4096]{1,0:T(8,128)(2,1)S(1)}, bf16[32,4096]{1,0:T(8,128)(2,1)S(1)}, u32[]{:S(2)}, u32[]{:S(2)}) collective-permute-start(bf16[32,4096]{1,0:T(8,128)(2,1)S(1)} %collective-permute-done.4.refs_2_), channel_id=1, source_target_pairs={{0,224},{32,0},{64,32},{96,64},{128,96},{160,128},{192,160},{224,1... | collective-permute-start | bytes 786440 | tf_op jit(solution)/shard_map/ppermute | solution.py:26
  30.8 2.9 %collective-permute-done.6.refs_4_ = bf16[32,4096]{1,0:T(8,128)(2,1)S(1)} collective-permute-done((bf16[32,4096]{1,0:T(8,128)(2,1)S(1)}, bf16[32,4096]{1,0:T(8,128)(2,1)S(1)}, u32[]{:S(2)}, u32[]{:S(2)}) %collective-permute-start.6) | collective-permute-done | bytes 262176 | tf_op jit(solution)/shard_map/ppermute | solution.py:26
  33.8 3.7 %collective-permute-start.8 = (bf16[32,4096]{1,0:T(8,128)(2,1)S(1)}, bf16[32,4096]{1,0:T(8,128)(2,1)S(1)}, u32[]{:S(2)}, u32[]{:S(2)}) collective-permute-start(bf16[32,4096]{1,0:T(8,128)(2,1)S(1)} %collective-permute-done.6.refs_4_), channel_id=1, source_target_pairs={{0,224},{32,0},{64,32},{96,64},{128,96},{160,128},{192,160},{224,1... | collective-permute-start | bytes 786440 | tf_op jit(solution)/shard_map/ppermute | solution.py:26
  39.1 1.9 copy-done
  41.7 2.5 shard_map.91.first_ref
  45.3 2.2 shard_map.92
  47.5 1.9 all_gather.3.refs_0_
  51.4 3.6 %collective-permute-done.10.refs_0_ = bf16[512,128]{1,0:T(8,128)(2,1)S(1)} collective-permute-done((bf16[512,128]{1,0:T(8,128)(2,1)S(1)}, bf16[512,128]{1,0:T(8,128)(2,1)S(1)}, u32[]{:S(2)}, u32[]{:S(2)}) %collective-permute-start.10) | collective-permute-done | bytes 131104 | tf_op jit(solution)/shard_map/ppermute | solution.py:26
  55.0 2.1 collective-permute-start.14
  57.1 4.5 %shard_map.94 = (bf16[144,512]{1,0:T(8,128)(2,1)S(1)}, bf16[144,512]{1,0:T(8,128)(2,1)S(1)}) custom-call(s32[8,8]{1,0:T(8,128)S(1)} %stack.41.table_ref, bf16[256,128]{1,0:T(8,128)(2,1)S(1)} %get-tuple-element.30.k_ref, bf16[256,128]{1,0:T(8,128)(2,1)S(1)} %get-tuple-element.31.v_ref, bf16[2,1024,256]{2,1,0:T(8,128)(2,1)S(1)} %bitcast.17, ...), custom_call_target="tpu_custom_call" | custom-call | flops 671088640 | tf_op jit(solution)/shard_map/pallas_call | solution.py:38
  61.7 1.5 collective-permute-start.12
  64.2 2.6 %shard_map.95 = bf16[144,512]{1,0:T(8,128)(2,1)S(1)} custom-call(s32[8,8]{1,0:T(8,128)S(1)} %stack.41.table_ref, bf16[256,128]{1,0:T(8,128)(2,1)S(1)} %get-tuple-element.30.k_ref, bf16[256,128]{1,0:T(8,128)(2,1)S(1)} %get-tuple-element.31.v_ref, bf16[2,1024,256]{2,1,0:T(8,128)(2,1)S(1)} %bitcast.18, bf16[512,128]{1,0:T(8,128)(2,1)S(1)} %collective-permute-done.14.refs_0_), custom_call_target="tpu_custom_call" | custom-call | flops 335544320 | tf_op jit(solution)/shard_map/pallas_call | solution.py:38
  67.6 2.7 %collective-permute-start.15 = (bf16[144,512]{1,0:T(8,128)(2,1)S(1)}, bf16[144,512]{1,0:T(8,128)(2,1)S(1)}, u32[]{:S(2)}, u32[]{:S(2)}) collective-permute-start(bf16[144,512]{1,0:T(8,128)(2,1)S(1)} %shard_map.95), channel_id=1, source_target_pairs={{0,4},{2,6},{4,0},{6,2},{1,5},{3,7},{5,1},{7,3},{8,12},{10,14},{12... | collective-permute-start | bytes 442376 | tf_op jit(solution)/shard_map/ppermute | solution.py:26
  70.2 2.6 %shard_map.93.refs_0_ = bf16[144,512]{1,0:T(8,128)(2,1)S(1)} custom-call(s32[8,8]{1,0:T(8,128)S(1)} %stack.41.table_ref, bf16[256,128]{1,0:T(8,128)(2,1)S(1)} %get-tuple-element.30.k_ref, bf16[256,128]{1,0:T(8,128)(2,1)S(1)} %get-tuple-element.31.v_ref, bf16[2,1024,256]{2,1,0:T(8,128)(2,1)S(1)} %bitcast.19, bf16[512,128]{1,0:T(8,128)(2,1)S(1)} %all_gather.3.refs_0_), custom_call_target="tpu_custom_call" | custom-call | flops 335544320 | tf_op jit(solution)/shard_map/pallas_call | solution.py:38
  78.6 1.5 pad_maximum_fusion.near_ref
  82.5 1.4 collective-permute-start.22
  83.8 3.9 %all-to-all-start = ((bf16[4,64,128]{2,1,0:T(8,128)(2,1)}), bf16[4,64,128]{2,1,0:T(8,128)(2,1)S(1)}, u32[]{:S(2)}, u32[]{:S(2)}) async-start(bf16[4,64,128]{2,1,0:T(8,128)(2,1)} %shard_map.97), calls=%async_computation | async-start | bytes 131072 | tf_op jit(solution)/shard_map/all_to_all | solution.py:380
  87.8 18.9 %collective-permute-done.20.refs_1_ = bf16[128,4096]{1,0:T(8,128)(2,1)} collective-permute-done((bf16[128,4096]{1,0:T(8,128)(2,1)}, bf16[128,4096]{1,0:T(8,128)(2,1)}, u32[]{:S(2)}, u32[]{:S(2)}) %collective-permute-start.20) | collective-permute-done | bytes 1048608 | tf_op jit(solution)/shard_map/ppermute | solution.py:26
  106.7 2.7 %collective-permute-done.21.refs_2_ = bf16[128,4096]{1,0:T(8,128)(2,1)} collective-permute-done((bf16[128,4096]{1,0:T(8,128)(2,1)}, bf16[128,4096]{1,0:T(8,128)(2,1)}, u32[]{:S(2)}, u32[]{:S(2)}) %collective-permute-start.21) | collective-permute-done | bytes 1048608 | tf_op jit(solution)/shard_map/ppermute | solution.py:26
  109.4 21.8 %collective-permute-done.22.refs_3_ = bf16[128,4096]{1,0:T(8,128)(2,1)} collective-permute-done((bf16[128,4096]{1,0:T(8,128)(2,1)}, bf16[128,4096]{1,0:T(8,128)(2,1)}, u32[]{:S(2)}, u32[]{:S(2)}) %collective-permute-start.22) | collective-permute-done | bytes 1048608 | tf_op jit(solution)/shard_map/ppermute | solution.py:26
  131.6 3.4 %shard_map.98 = bf16[8,8,4096]{2,1,0:T(8,128)(2,1)S(1)} custom-call(s32[8,8]{1,0:T(8,128)S(1)} %stack.41.table_ref, bf16[4,64,128]{2,1,0:T(8,128)(2,1)S(1)} %all-to-all-done.heads_ref, bf16[128,4096]{1,0:T(8,128)(2,1)} %refs_0_, bf16[128,4096]{1,0:T(8,128)(2,1)} %collective-permute-done.20.refs_1_, bf16[128,4096]{1,0:T(8,128)(2,1)} %collective-permute-done.21.refs_2_, ...), custom_call_target="tpu_custom_call" | custom-call | tf_op jit(solution)/shard_map/pallas_call | solution.py:38
  135.7 5.6 %all-to-all-start.1 = ((bf16[8,8,4096]{2,1,0:T(8,128)(2,1)}), bf16[8,8,4096]{2,1,0:T(8,128)(2,1)S(1)}, u32[]{:S(2)}, u32[]{:S(2)}) async-start(bf16[8,8,4096]{2,1,0:T(8,128)(2,1)} %copy-done.2), calls=%async_computation.1 | async-start | bytes 1048576 | tf_op jit(solution)/shard_map/all_to_all | solution.py:380
  142.5 2.0 collective-permute-start.35
  144.5 1.8 collective-permute-start.34
  146.3 12.5 %all-to-all-done.1.terms_ref = bf16[8,8,4096]{2,1,0:T(8,128)(2,1)S(1)} async-done(((bf16[8,8,4096]{2,1,0:T(8,128)(2,1)}), bf16[8,8,4096]{2,1,0:T(8,128)(2,1)S(1)}, u32[]{:S(2)}, u32[]{:S(2)}) %all-to-all-start.1) | async-done | bytes 524320 | tf_op jit(solution)/shard_map/all_to_all | solution.py:380
  159.7 1.6 collective-permute-start.25
  162.4 1.5 pad_maximum_fusion.1.refs_0_
  164.4 1.5 collective-permute-done.25
  167.4 2.8 %collective-permute-start.28 = (bf16[32,4096]{1,0:T(8,128)(2,1)S(1)}, bf16[32,4096]{1,0:T(8,128)(2,1)S(1)}, u32[]{:S(2)}, u32[]{:S(2)}) collective-permute-start(bf16[32,4096]{1,0:T(8,128)(2,1)S(1)} %pad_maximum_fusion.3.refs_0_), channel_id=1, source_target_pairs={{0,224},{32,0},{64,32},{96,64},{128,96},{160,128},{192,160},{224,1... | collective-permute-start | bytes 786440 | tf_op jit(solution)/shard_map/ppermute | solution.py:26
  170.3 5.8 %collective-permute-done.27.refs_1_ = bf16[32,4096]{1,0:T(8,128)(2,1)S(1)} collective-permute-done((bf16[32,4096]{1,0:T(8,128)(2,1)S(1)}, bf16[32,4096]{1,0:T(8,128)(2,1)S(1)}, u32[]{:S(2)}, u32[]{:S(2)}) %collective-permute-start.27) | collective-permute-done | bytes 262176 | tf_op jit(solution)/shard_map/ppermute | solution.py:26
  176.0 3.2 %collective-permute-start.30 = (bf16[32,4096]{1,0:T(8,128)(2,1)S(1)}, bf16[32,4096]{1,0:T(8,128)(2,1)S(1)}, u32[]{:S(2)}, u32[]{:S(2)}) collective-permute-start(bf16[32,4096]{1,0:T(8,128)(2,1)S(1)} %collective-permute-done.28.refs_2_), channel_id=1, source_target_pairs={{0,224},{32,0},{64,32},{96,64},{128,96},{160,128},{192,160},{224,1... | collective-permute-start | bytes 786440 | tf_op jit(solution)/shard_map/ppermute | solution.py:26
  179.3 4.9 %collective-permute-done.29.refs_3_ = bf16[32,4096]{1,0:T(8,128)(2,1)S(1)} collective-permute-done((bf16[32,4096]{1,0:T(8,128)(2,1)S(1)}, bf16[32,4096]{1,0:T(8,128)(2,1)S(1)}, u32[]{:S(2)}, u32[]{:S(2)}) %collective-permute-start.29) | collective-permute-done | bytes 262176 | tf_op jit(solution)/shard_map/ppermute | solution.py:26
  184.2 3.2 %collective-permute-start.32 = (bf16[32,4096]{1,0:T(8,128)(2,1)S(1)}, bf16[32,4096]{1,0:T(8,128)(2,1)S(1)}, u32[]{:S(2)}, u32[]{:S(2)}) collective-permute-start(bf16[32,4096]{1,0:T(8,128)(2,1)S(1)} %collective-permute-done.30.refs_4_), channel_id=1, source_target_pairs={{0,224},{32,0},{64,32},{96,64},{128,96},{160,128},{192,160},{224,1... | collective-permute-start | bytes 786440 | tf_op jit(solution)/shard_map/ppermute | solution.py:26
  187.4 4.3 %collective-permute-done.31.refs_5_ = bf16[32,4096]{1,0:T(8,128)(2,1)S(1)} collective-permute-done((bf16[32,4096]{1,0:T(8,128)(2,1)S(1)}, bf16[32,4096]{1,0:T(8,128)(2,1)S(1)}, u32[]{:S(2)}, u32[]{:S(2)}) %collective-permute-start.31) | collective-permute-done | bytes 262176 | tf_op jit(solution)/shard_map/ppermute | solution.py:26
  191.8 7.6 %collective-permute-done.33.refs_7_ = bf16[32,4096]{1,0:T(8,128)(2,1)S(1)} collective-permute-done((bf16[32,4096]{1,0:T(8,128)(2,1)S(1)}, bf16[32,4096]{1,0:T(8,128)(2,1)S(1)}, u32[]{:S(2)}, u32[]{:S(2)}) %collective-permute-start.33) | collective-permute-done | bytes 262176 | tf_op jit(solution)/shard_map/ppermute | solution.py:26
  199.4 5.1 %shard_map.100.x_ref = bf16[256,344]{1,0:T(8,128)(2,1)S(1)} custom-call(s32[8,8]{1,0:T(8,128)S(1)} %stack.41.table_ref, bf16[4,2,344,512]{3,2,1,0:T(8,128)(2,1)S(1)} %pad_maximum_fusion.near_ref, bf16[4,2,344,512]{3,2,1,0:T(8,128)(2,1)} %collective-permute-done.23.far_ref, bf16[32,4096]{1,0:T(8,128)(2,1)S(1)} %pad_maximum_fusion.3.refs_0_, ...), custom_call_target="tpu_custom_call" | custom-call | flops 1442840576 | tf_op jit(solution)/shard_map/pallas_call | solution.py:38
  204.5 3.0 %shard_map.101 = (bf16[64,4096]{1,0:T(8,128)(2,1)S(1)}, bf16[64,4096]{1,0:T(8,128)(2,1)S(1)}, bf16[64,4096]{1,0:T(8,128)(2,1)S(1)}, bf16[64,4096]{1,0:T(8,128)(2,1)S(1)}) custom-call(s32[8,8]{1,0:T(8,128)S(1)} %stack.41.table_ref, bf16[256,344]{1,0:T(8,128)(2,1)S(1)} %shard_map.100.x_ref, bf16[4,344,512]{2,1,0:T(8,128)(2,1)S(1)} %pad_maximum_fusion.1.refs_0_, ...), custom_call_target="tpu_custom_call" | custom-call | tf_op jit(solution)/shard_map/pallas_call | solution.py:38
  210.6 11.8 %collective-permute-done.38.refs_1_ = bf16[64,4096]{1,0:T(8,128)(2,1)S(1)} collective-permute-done((bf16[64,4096]{1,0:T(8,128)(2,1)S(1)}, bf16[64,4096]{1,0:T(8,128)(2,1)S(1)}, u32[]{:S(2)}, u32[]{:S(2)}) %collective-permute-start.38) | collective-permute-done | bytes 524320 | tf_op jit(solution)/shard_map/ppermute | solution.py:26
  222.3 1.9 collective-permute-done.39.refs_2_
  224.2 5.6 %collective-permute-done.40.refs_3_ = bf16[64,4096]{1,0:T(8,128)(2,1)S(1)} collective-permute-done((bf16[64,4096]{1,0:T(8,128)(2,1)S(1)}, bf16[64,4096]{1,0:T(8,128)(2,1)S(1)}, u32[]{:S(2)}, u32[]{:S(2)}) %collective-permute-start.40) | collective-permute-done | bytes 524320 | tf_op jit(solution)/shard_map/ppermute | solution.py:26
  230.6 23.3 %all_to_all.15 = bf16[8,8,4096]{2,1,0:T(8,128)(2,1)S(1)} all-to-all(bf16[8,8,4096]{2,1,0:T(8,128)(2,1)S(1)} %shard_map.102), channel_id=1, replica_groups=mesh['z'=8,'y'=4,'x'=4,'c'=2] {'z'}, dimensions={0} | all-to-all | bytes 1048576 | tf_op jit(solution)/shard_map/all_to_all | solution.py:380
  (81 shorter events, 33.1 us)
Async XLA Ops:
  0.0 5.5 %collective-permute-start.2 = (bf16[8,4096]{1,0:T(8,128)(2,1)}, bf16[8,4096]{1,0:T(8,128)(2,1)S(1)}, u32[]{:S(2)}, u32[]{:S(2)}) collective-permute-start(bf16[8,4096]{1,0:T(8,128)(2,1)} %hidden_ref.1), channel_id=1, source_target_pairs={{0,24},{8,0},{16,8},{24,16},{1,25},{9,1},{17,9},{25,17},{2,26},{10... | collective-permute-start | bytes 196616 | tf_op jit(solution)/shard_map/ppermute | solution.py:26
  3.0 6.0 %collective-permute-start.1 = (bf16[8,4096]{1,0:T(8,128)(2,1)}, bf16[8,4096]{1,0:T(8,128)(2,1)S(1)}, u32[]{:S(2)}, u32[]{:S(2)}) collective-permute-start(bf16[8,4096]{1,0:T(8,128)(2,1)} %hidden_ref.1), channel_id=1, source_target_pairs={{0,16},{8,24},{16,0},{24,8},{1,17},{9,25},{17,1},{25,9},{2,18},{10... | collective-permute-start | bytes 196616 | tf_op jit(solution)/shard_map/ppermute | solution.py:26
  3.6 6.1 %collective-permute-start = (bf16[8,4096]{1,0:T(8,128)(2,1)}, bf16[8,4096]{1,0:T(8,128)(2,1)S(1)}, u32[]{:S(2)}, u32[]{:S(2)}) collective-permute-start(bf16[8,4096]{1,0:T(8,128)(2,1)} %hidden_ref.1), channel_id=1, source_target_pairs={{0,8},{8,16},{16,24},{24,0},{1,9},{9,17},{17,25},{25,1},{2,10},{10... | collective-permute-start | bytes 196616 | tf_op jit(solution)/shard_map/ppermute | solution.py:26
  10.6 10.8 %collective-permute-start.3 = (bf16[32,4096]{1,0:T(8,128)(2,1)S(1)}, bf16[32,4096]{1,0:T(8,128)(2,1)S(1)}, u32[]{:S(2)}, u32[]{:S(2)}) collective-permute-start(bf16[32,4096]{1,0:T(8,128)(2,1)S(1)} %pad_maximum_fusion.2.refs_0_), channel_id=1, source_target_pairs={{0,32},{32,64},{64,96},{96,128},{128,160},{160,192},{192,224},{224... | collective-permute-start | bytes 786440 | tf_op jit(solution)/shard_map/ppermute | solution.py:26
  12.6 13.6 %collective-permute-start.4 = (bf16[32,4096]{1,0:T(8,128)(2,1)S(1)}, bf16[32,4096]{1,0:T(8,128)(2,1)S(1)}, u32[]{:S(2)}, u32[]{:S(2)}) collective-permute-start(bf16[32,4096]{1,0:T(8,128)(2,1)S(1)} %pad_maximum_fusion.2.refs_0_), channel_id=1, source_target_pairs={{0,224},{32,0},{64,32},{96,64},{128,96},{160,128},{192,160},{224,1... | collective-permute-start | bytes 786440 | tf_op jit(solution)/shard_map/ppermute | solution.py:26
  21.4 8.0 %collective-permute-start.5 = (bf16[32,4096]{1,0:T(8,128)(2,1)S(1)}, bf16[32,4096]{1,0:T(8,128)(2,1)S(1)}, u32[]{:S(2)}, u32[]{:S(2)}) collective-permute-start(bf16[32,4096]{1,0:T(8,128)(2,1)S(1)} %collective-permute-done.3.refs_1_), channel_id=1, source_target_pairs={{0,32},{32,64},{64,96},{96,128},{128,160},{160,192},{192,224},{224... | collective-permute-start | bytes 786440 | tf_op jit(solution)/shard_map/ppermute | solution.py:26
  21.4 56.3 %collective-permute-start.17 = (bf16[2,344,512]{2,1,0:T(8,128)(2,1)}, bf16[2,344,512]{2,1,0:T(8,128)(2,1)S(1)}, u32[]{:S(2)}, u32[]{:S(2)}) collective-permute-start(bf16[2,344,512]{2,1,0:T(8,128)(2,1)} %bitcast.23), channel_id=1, source_target_pairs={{0,2},{2,4},{4,6},{6,0},{1,3},{3,5},{5,7},{7,1},{8,10},{10,12},{12... | collective-permute-start | bytes 2113544 | tf_op jit(solution)/shard_map/ppermute | solution.py:26
  22.9 54.8 %collective-permute-start.18 = (bf16[2,344,512]{2,1,0:T(8,128)(2,1)}, bf16[2,344,512]{2,1,0:T(8,128)(2,1)S(1)}, u32[]{:S(2)}, u32[]{:S(2)}) collective-permute-start(bf16[2,344,512]{2,1,0:T(8,128)(2,1)} %bitcast.24), channel_id=1, source_target_pairs={{0,4},{2,6},{4,0},{6,2},{1,5},{3,7},{5,1},{7,3},{8,12},{10,14},{12... | collective-permute-start | bytes 2113544 | tf_op jit(solution)/shard_map/ppermute | solution.py:26
  24.0 53.7 %collective-permute-start.19 = (bf16[2,344,512]{2,1,0:T(8,128)(2,1)}, bf16[2,344,512]{2,1,0:T(8,128)(2,1)}, u32[]{:S(2)}, u32[]{:S(2)}) collective-permute-start(bf16[2,344,512]{2,1,0:T(8,128)(2,1)} %bitcast.25), channel_id=1, source_target_pairs={{0,6},{2,0},{4,2},{6,4},{1,7},{3,1},{5,3},{7,5},{8,14},{10,8},{12,... | collective-permute-start | bytes 2113544 | tf_op jit(solution)/shard_map/ppermute | solution.py:26
  26.1 7.6 %collective-permute-start.6 = (bf16[32,4096]{1,0:T(8,128)(2,1)S(1)}, bf16[32,4096]{1,0:T(8,128)(2,1)S(1)}, u32[]{:S(2)}, u32[]{:S(2)}) collective-permute-start(bf16[32,4096]{1,0:T(8,128)(2,1)S(1)} %collective-permute-done.4.refs_2_), channel_id=1, source_target_pairs={{0,224},{32,0},{64,32},{96,64},{128,96},{160,128},{192,160},{224,1... | collective-permute-start | bytes 786440 | tf_op jit(solution)/shard_map/ppermute | solution.py:26
  29.4 8.4 %collective-permute-start.7 = (bf16[32,4096]{1,0:T(8,128)(2,1)S(1)}, bf16[32,4096]{1,0:T(8,128)(2,1)S(1)}, u32[]{:S(2)}, u32[]{:S(2)}) collective-permute-start(bf16[32,4096]{1,0:T(8,128)(2,1)S(1)} %collective-permute-done.5.refs_3_), channel_id=1, source_target_pairs={{0,32},{32,64},{64,96},{96,128},{128,160},{160,192},{192,224},{224... | collective-permute-start | bytes 786440 | tf_op jit(solution)/shard_map/ppermute | solution.py:26
  33.8 10.4 %collective-permute-start.8 = (bf16[32,4096]{1,0:T(8,128)(2,1)S(1)}, bf16[32,4096]{1,0:T(8,128)(2,1)S(1)}, u32[]{:S(2)}, u32[]{:S(2)}) collective-permute-start(bf16[32,4096]{1,0:T(8,128)(2,1)S(1)} %collective-permute-done.6.refs_4_), channel_id=1, source_target_pairs={{0,224},{32,0},{64,32},{96,64},{128,96},{160,128},{192,160},{224,1... | collective-permute-start | bytes 786440 | tf_op jit(solution)/shard_map/ppermute | solution.py:26
  37.7 7.6 %collective-permute-start.9 = (bf16[32,4096]{1,0:T(8,128)(2,1)S(1)}, bf16[32,4096]{1,0:T(8,128)(2,1)S(1)}, u32[]{:S(2)}, u32[]{:S(2)}) collective-permute-start(bf16[32,4096]{1,0:T(8,128)(2,1)S(1)} %collective-permute-done.7.refs_0_), channel_id=1, source_target_pairs={{0,32},{32,64},{64,96},{96,128},{128,160},{160,192},{192,224},{224... | collective-permute-start | bytes 786440 | tf_op jit(solution)/shard_map/ppermute | solution.py:26
  39.1 1.9 copy-start
  44.2 13.0 %copy-start.1 = (bf16[2,1024,1,256]{3,1,2,0:T(8,128)(2,1)S(1)}, bf16[2,1024,1,256]{3,1,2,0:T(8,128)(2,1)}, u32[]{:S(2)}) copy-start(bf16[2,1024,1,256]{3,1,2,0:T(8,128)(2,1)} %param.12) | copy-start | bytes 3145732
  49.4 5.6 %collective-permute-start.10 = (bf16[512,128]{1,0:T(8,128)(2,1)S(1)}, bf16[512,128]{1,0:T(8,128)(2,1)S(1)}, u32[]{:S(2)}, u32[]{:S(2)}) collective-permute-start(bf16[512,128]{1,0:T(8,128)(2,1)S(1)} %all_gather.3.refs_0_), channel_id=1, source_target_pairs={{0,2},{2,4},{4,6},{6,0},{1,3},{3,5},{5,7},{7,1},{8,10},{10,12},{12... | collective-permute-start | bytes 393224 | tf_op jit(solution)/shard_map/ppermute | solution.py:26
  50.4 6.8 %collective-permute-start.11 = (bf16[512,128]{1,0:T(8,128)(2,1)S(1)}, bf16[512,128]{1,0:T(8,128)(2,1)S(1)}, u32[]{:S(2)}, u32[]{:S(2)}) collective-permute-start(bf16[512,128]{1,0:T(8,128)(2,1)S(1)} %all_gather.3.refs_0_), channel_id=1, source_target_pairs={{0,6},{2,0},{4,2},{6,4},{1,7},{3,1},{5,3},{7,5},{8,14},{10,8},{12,... | collective-permute-start | bytes 393224 | tf_op jit(solution)/shard_map/ppermute | solution.py:26
  55.0 8.2 %collective-permute-start.14 = (bf16[512,128]{1,0:T(8,128)(2,1)S(1)}, bf16[512,128]{1,0:T(8,128)(2,1)S(1)}, u32[]{:S(2)}, u32[]{:S(2)}) collective-permute-start(bf16[512,128]{1,0:T(8,128)(2,1)S(1)} %all_gather.3.refs_0_), channel_id=1, source_target_pairs={{0,4},{2,6},{4,0},{6,2},{1,5},{3,7},{5,1},{7,3},{8,12},{10,14},{12... | collective-permute-start | bytes 393224 | tf_op jit(solution)/shard_map/ppermute | solution.py:26
  57.1 21.4 %copy-start.6 = (bf16[512,2,344]{0,2,1:T(8,128)(2,1)S(1)}, bf16[512,2,344]{0,2,1:T(8,128)(2,1)}, u32[]{:S(2)}) copy-start(bf16[512,2,344]{0,2,1:T(8,128)(2,1)} %param.16) | copy-start | bytes 2113540
  61.7 5.9 %collective-permute-start.12 = (bf16[144,512]{1,0:T(8,128)(2,1)S(1)}, bf16[144,512]{1,0:T(8,128)(2,1)S(1)}, u32[]{:S(2)}, u32[]{:S(2)}) collective-permute-start(bf16[144,512]{1,0:T(8,128)(2,1)S(1)} %get-tuple-element.33), channel_id=1, source_target_pairs={{0,6},{2,0},{4,2},{6,4},{1,7},{3,1},{5,3},{7,5},{8,14},{10,8},{12,... | collective-permute-start | bytes 442376 | tf_op jit(solution)/shard_map/ppermute | solution.py:26
  63.2 9.6 %collective-permute-start.13 = (bf16[144,512]{1,0:T(8,128)(2,1)S(1)}, bf16[144,512]{1,0:T(8,128)(2,1)S(1)}, u32[]{:S(2)}, u32[]{:S(2)}) collective-permute-start(bf16[144,512]{1,0:T(8,128)(2,1)S(1)} %get-tuple-element.34), channel_id=1, source_target_pairs={{0,2},{2,4},{4,6},{6,0},{1,3},{3,5},{5,7},{7,1},{8,10},{10,12},{12... | collective-permute-start | bytes 442376 | tf_op jit(solution)/shard_map/ppermute | solution.py:26
  67.6 6.6 %collective-permute-start.15 = (bf16[144,512]{1,0:T(8,128)(2,1)S(1)}, bf16[144,512]{1,0:T(8,128)(2,1)S(1)}, u32[]{:S(2)}, u32[]{:S(2)}) collective-permute-start(bf16[144,512]{1,0:T(8,128)(2,1)S(1)} %shard_map.95), channel_id=1, source_target_pairs={{0,4},{2,6},{4,0},{6,2},{1,5},{3,7},{5,1},{7,3},{8,12},{10,14},{12... | collective-permute-start | bytes 442376 | tf_op jit(solution)/shard_map/ppermute | solution.py:26
  75.0 1.4 collective-permute-start.16
  80.1 79.5 %collective-permute-start.23 = (bf16[4,2,344,512]{3,2,1,0:T(8,128)(2,1)S(1)}, bf16[4,2,344,512]{3,2,1,0:T(8,128)(2,1)}, u32[]{:S(2)}, u32[]{:S(2)}) collective-permute-start(bf16[4,2,344,512]{3,2,1,0:T(8,128)(2,1)S(1)} %pad_maximum_fusion.near_ref), channel_id=1, source_target_pairs={{0,1},{1,0},{2,3},{3,2},{4,5},{5,4},{6,7},{7,6},{8,9},{9,8},{10,11... | collective-permute-start | bytes 8454152 | tf_op jit(solution)/shard_map/ppermute | solution.py:26
  80.3 26.3 %collective-permute-start.20 = (bf16[128,4096]{1,0:T(8,128)(2,1)}, bf16[128,4096]{1,0:T(8,128)(2,1)}, u32[]{:S(2)}, u32[]{:S(2)}) collective-permute-start(bf16[128,4096]{1,0:T(8,128)(2,1)} %refs_0_), channel_id=1, source_target_pairs={{0,24},{8,0},{16,8},{24,16},{1,25},{9,1},{17,9},{25,17},{2,26},{10... | collective-permute-start | bytes 3145736 | tf_op jit(solution)/shard_map/ppermute | solution.py:26
  81.5 27.9 %collective-permute-start.21 = (bf16[128,4096]{1,0:T(8,128)(2,1)}, bf16[128,4096]{1,0:T(8,128)(2,1)}, u32[]{:S(2)}, u32[]{:S(2)}) collective-permute-start(bf16[128,4096]{1,0:T(8,128)(2,1)} %refs_0_), channel_id=1, source_target_pairs={{0,16},{8,24},{16,0},{24,8},{1,17},{9,25},{17,1},{25,9},{2,18},{10... | collective-permute-start | bytes 3145736 | tf_op jit(solution)/shard_map/ppermute | solution.py:26
  82.5 48.7 %collective-permute-start.22 = (bf16[128,4096]{1,0:T(8,128)(2,1)}, bf16[128,4096]{1,0:T(8,128)(2,1)}, u32[]{:S(2)}, u32[]{:S(2)}) collective-permute-start(bf16[128,4096]{1,0:T(8,128)(2,1)} %refs_0_), channel_id=1, source_target_pairs={{0,8},{8,16},{16,24},{24,0},{1,9},{9,17},{17,25},{25,1},{2,10},{10... | collective-permute-start | bytes 3145736 | tf_op jit(solution)/shard_map/ppermute | solution.py:26
  83.8 47.7 %all-to-all-start = ((bf16[4,64,128]{2,1,0:T(8,128)(2,1)}), bf16[4,64,128]{2,1,0:T(8,128)(2,1)S(1)}, u32[]{:S(2)}, u32[]{:S(2)}) async-start(bf16[4,64,128]{2,1,0:T(8,128)(2,1)} %shard_map.97), calls=%async_computation | async-start | bytes 131072 | tf_op jit(solution)/shard_map/all_to_all | solution.py:380
  87.8 71.0 %copy-start.3 = (bf16[8,4096]{1,0:T(8,128)(2,1)S(1)}, bf16[8,4096]{1,0:T(8,128)(2,1)}, u32[]{:S(2)}) copy-start(bf16[8,4096]{1,0:T(8,128)(2,1)} %hidden_ref.1) | copy-start | bytes 196612
  87.8 71.0 %copy-start.5 = (f32[4096]{0:T(1024)S(1)}, f32[4096]{0:T(1024)}, u32[]{:S(2)}) copy-start(f32[4096]{0:T(1024)} %param.15) | copy-start | bytes 49156
  135.7 23.0 %all-to-all-start.1 = ((bf16[8,8,4096]{2,1,0:T(8,128)(2,1)}), bf16[8,8,4096]{2,1,0:T(8,128)(2,1)S(1)}, u32[]{:S(2)}, u32[]{:S(2)}) async-start(bf16[8,8,4096]{2,1,0:T(8,128)(2,1)} %copy-done.2), calls=%async_computation.1 | async-start | bytes 1048576 | tf_op jit(solution)/shard_map/all_to_all | solution.py:380
  141.3 20.0 %collective-permute-start.36 = (bf16[344,512]{1,0:T(8,128)(2,1)}, bf16[344,512]{1,0:T(8,128)(2,1)}, u32[]{:S(2)}, u32[]{:S(2)}) collective-permute-start(bf16[344,512]{1,0:T(8,128)(2,1)} %param.17), channel_id=1, source_target_pairs={{0,6},{2,0},{4,2},{6,4},{1,7},{3,1},{5,3},{7,5},{8,14},{10,8},{12,... | collective-permute-start | bytes 1056776 | tf_op jit(solution)/shard_map/ppermute | solution.py:26
  142.5 19.9 %collective-permute-start.35 = (bf16[344,512]{1,0:T(8,128)(2,1)}, bf16[344,512]{1,0:T(8,128)(2,1)}, u32[]{:S(2)}, u32[]{:S(2)}) collective-permute-start(bf16[344,512]{1,0:T(8,128)(2,1)} %param.17), channel_id=1, source_target_pairs={{0,4},{2,6},{4,0},{6,2},{1,5},{3,7},{5,1},{7,3},{8,12},{10,14},{12... | collective-permute-start | bytes 1056776 | tf_op jit(solution)/shard_map/ppermute | solution.py:26
  144.5 17.9 %collective-permute-start.34 = (bf16[344,512]{1,0:T(8,128)(2,1)}, bf16[344,512]{1,0:T(8,128)(2,1)}, u32[]{:S(2)}, u32[]{:S(2)}) collective-permute-start(bf16[344,512]{1,0:T(8,128)(2,1)} %param.17), channel_id=1, source_target_pairs={{0,2},{2,4},{4,6},{6,0},{1,3},{3,5},{5,7},{7,1},{8,10},{10,12},{12... | collective-permute-start | bytes 1056776 | tf_op jit(solution)/shard_map/ppermute | solution.py:26
  159.6 4.8 %collective-permute-start.26 = (bf16[8,4096]{1,0:T(8,128)(2,1)S(1)}, bf16[8,4096]{1,0:T(8,128)(2,1)S(1)}, u32[]{:S(2)}, u32[]{:S(2)}) collective-permute-start(bf16[8,4096]{1,0:T(8,128)(2,1)S(1)} %get-tuple-element.47), channel_id=1, source_target_pairs={{0,24},{8,0},{16,8},{24,16},{1,25},{9,1},{17,9},{25,17},{2,26},{10... | collective-permute-start | bytes 196616 | tf_op jit(solution)/shard_map/ppermute | solution.py:26
  159.7 6.1 %collective-permute-start.25 = (bf16[8,4096]{1,0:T(8,128)(2,1)S(1)}, bf16[8,4096]{1,0:T(8,128)(2,1)S(1)}, u32[]{:S(2)}, u32[]{:S(2)}) collective-permute-start(bf16[8,4096]{1,0:T(8,128)(2,1)S(1)} %get-tuple-element.47), channel_id=1, source_target_pairs={{0,16},{8,24},{16,0},{24,8},{1,17},{9,25},{17,1},{25,9},{2,18},{10... | collective-permute-start | bytes 196616 | tf_op jit(solution)/shard_map/ppermute | solution.py:26
  161.3 5.6 %collective-permute-start.24 = (bf16[8,4096]{1,0:T(8,128)(2,1)S(1)}, bf16[8,4096]{1,0:T(8,128)(2,1)S(1)}, u32[]{:S(2)}, u32[]{:S(2)}) collective-permute-start(bf16[8,4096]{1,0:T(8,128)(2,1)S(1)} %get-tuple-element.47), channel_id=1, source_target_pairs={{0,8},{8,16},{16,24},{24,0},{1,9},{9,17},{17,25},{25,1},{2,10},{10... | collective-permute-start | bytes 196616 | tf_op jit(solution)/shard_map/ppermute | solution.py:26
  163.9 40.6 %collective-permute-start.37 = (bf16[4,344,512]{2,1,0:T(8,128)(2,1)S(1)}, bf16[4,344,512]{2,1,0:T(8,128)(2,1)S(1)}, u32[]{:S(2)}, u32[]{:S(2)}) collective-permute-start(bf16[4,344,512]{2,1,0:T(8,128)(2,1)S(1)} %pad_maximum_fusion.1.refs_0_), channel_id=1, source_target_pairs={{0,1},{1,0},{2,3},{3,2},{4,5},{5,4},{6,7},{7,6},{8,9},{9,8},{10,11... | collective-permute-start | bytes 4227080 | tf_op jit(solution)/shard_map/ppermute | solution.py:26
  167.0 9.1 %collective-permute-start.27 = (bf16[32,4096]{1,0:T(8,128)(2,1)S(1)}, bf16[32,4096]{1,0:T(8,128)(2,1)S(1)}, u32[]{:S(2)}, u32[]{:S(2)}) collective-permute-start(bf16[32,4096]{1,0:T(8,128)(2,1)S(1)} %pad_maximum_fusion.3.refs_0_), channel_id=1, source_target_pairs={{0,32},{32,64},{64,96},{96,128},{128,160},{160,192},{192,224},{224... | collective-permute-start | bytes 786440 | tf_op jit(solution)/shard_map/ppermute | solution.py:26
  167.4 8.6 %collective-permute-start.28 = (bf16[32,4096]{1,0:T(8,128)(2,1)S(1)}, bf16[32,4096]{1,0:T(8,128)(2,1)S(1)}, u32[]{:S(2)}, u32[]{:S(2)}) collective-permute-start(bf16[32,4096]{1,0:T(8,128)(2,1)S(1)} %pad_maximum_fusion.3.refs_0_), channel_id=1, source_target_pairs={{0,224},{32,0},{64,32},{96,64},{128,96},{160,128},{192,160},{224,1... | collective-permute-start | bytes 786440 | tf_op jit(solution)/shard_map/ppermute | solution.py:26
  176.0 8.1 %collective-permute-start.29 = (bf16[32,4096]{1,0:T(8,128)(2,1)S(1)}, bf16[32,4096]{1,0:T(8,128)(2,1)S(1)}, u32[]{:S(2)}, u32[]{:S(2)}) collective-permute-start(bf16[32,4096]{1,0:T(8,128)(2,1)S(1)} %collective-permute-done.27.refs_1_), channel_id=1, source_target_pairs={{0,32},{32,64},{64,96},{96,128},{128,160},{160,192},{192,224},{224... | collective-permute-start | bytes 786440 | tf_op jit(solution)/shard_map/ppermute | solution.py:26
  176.0 8.1 %collective-permute-start.30 = (bf16[32,4096]{1,0:T(8,128)(2,1)S(1)}, bf16[32,4096]{1,0:T(8,128)(2,1)S(1)}, u32[]{:S(2)}, u32[]{:S(2)}) collective-permute-start(bf16[32,4096]{1,0:T(8,128)(2,1)S(1)} %collective-permute-done.28.refs_2_), channel_id=1, source_target_pairs={{0,224},{32,0},{64,32},{96,64},{128,96},{160,128},{192,160},{224,1... | collective-permute-start | bytes 786440 | tf_op jit(solution)/shard_map/ppermute | solution.py:26
  184.2 7.6 %collective-permute-start.31 = (bf16[32,4096]{1,0:T(8,128)(2,1)S(1)}, bf16[32,4096]{1,0:T(8,128)(2,1)S(1)}, u32[]{:S(2)}, u32[]{:S(2)}) collective-permute-start(bf16[32,4096]{1,0:T(8,128)(2,1)S(1)} %collective-permute-done.29.refs_3_), channel_id=1, source_target_pairs={{0,32},{32,64},{64,96},{96,128},{128,160},{160,192},{192,224},{224... | collective-permute-start | bytes 786440 | tf_op jit(solution)/shard_map/ppermute | solution.py:26
  184.2 7.6 %collective-permute-start.32 = (bf16[32,4096]{1,0:T(8,128)(2,1)S(1)}, bf16[32,4096]{1,0:T(8,128)(2,1)S(1)}, u32[]{:S(2)}, u32[]{:S(2)}) collective-permute-start(bf16[32,4096]{1,0:T(8,128)(2,1)S(1)} %collective-permute-done.30.refs_4_), channel_id=1, source_target_pairs={{0,224},{32,0},{64,32},{96,64},{128,96},{160,128},{192,160},{224,1... | collective-permute-start | bytes 786440 | tf_op jit(solution)/shard_map/ppermute | solution.py:26
  191.8 7.6 %collective-permute-start.33 = (bf16[32,4096]{1,0:T(8,128)(2,1)S(1)}, bf16[32,4096]{1,0:T(8,128)(2,1)S(1)}, u32[]{:S(2)}, u32[]{:S(2)}) collective-permute-start(bf16[32,4096]{1,0:T(8,128)(2,1)S(1)} %collective-permute-done.31.refs_5_), channel_id=1, source_target_pairs={{0,32},{32,64},{64,96},{96,128},{128,160},{160,192},{192,224},{224... | collective-permute-start | bytes 786440 | tf_op jit(solution)/shard_map/ppermute | solution.py:26
  207.5 14.9 %collective-permute-start.38 = (bf16[64,4096]{1,0:T(8,128)(2,1)S(1)}, bf16[64,4096]{1,0:T(8,128)(2,1)S(1)}, u32[]{:S(2)}, u32[]{:S(2)}) collective-permute-start(bf16[64,4096]{1,0:T(8,128)(2,1)S(1)} %get-tuple-element.50), channel_id=1, source_target_pairs={{0,24},{8,0},{16,8},{24,16},{1,25},{9,1},{17,9},{25,17},{2,26},{10... | collective-permute-start | bytes 1572872 | tf_op jit(solution)/shard_map/ppermute | solution.py:26
  208.5 15.8 %collective-permute-start.39 = (bf16[64,4096]{1,0:T(8,128)(2,1)S(1)}, bf16[64,4096]{1,0:T(8,128)(2,1)S(1)}, u32[]{:S(2)}, u32[]{:S(2)}) collective-permute-start(bf16[64,4096]{1,0:T(8,128)(2,1)S(1)} %get-tuple-element.51), channel_id=1, source_target_pairs={{0,16},{8,24},{16,0},{24,8},{1,17},{9,25},{17,1},{25,9},{2,18},{10... | collective-permute-start | bytes 1572872 | tf_op jit(solution)/shard_map/ppermute | solution.py:26
  209.4 20.4 %collective-permute-start.40 = (bf16[64,4096]{1,0:T(8,128)(2,1)S(1)}, bf16[64,4096]{1,0:T(8,128)(2,1)S(1)}, u32[]{:S(2)}, u32[]{:S(2)}) collective-permute-start(bf16[64,4096]{1,0:T(8,128)(2,1)S(1)} %get-tuple-element.52), channel_id=1, source_target_pairs={{0,8},{8,16},{16,24},{24,0},{1,9},{9,17},{17,25},{25,1},{2,10},{10... | collective-permute-start | bytes 1572872 | tf_op jit(solution)/shard_map/ppermute | solution.py:26
  (3 other events, 2.4 us)

commit v2 on v1

--- a/solution.py
+++ b/solution.py
@@ -34,14 +34,16 @@
     return lax.dot_general(a, b, (((ca,), (cb,)), ((), ())), preferred_element_type=F32)
 
 
-def run(kernel, table, arrays, outs, flops=0, limit=16, scratch=()):
+def run(kernel, table, arrays, outs, flops=0, limit=16, scratch=(), far=0, sems=0):
     return pl.pallas_call(
         kernel,
         in_specs=[pl.BlockSpec(memory_space=pltpu.SMEM)]
-        + [pl.BlockSpec(memory_space=pltpu.VMEM)] * len(arrays),
+        + [pl.BlockSpec(memory_space=pltpu.HBM)] * far
+        + [pl.BlockSpec(memory_space=pltpu.VMEM)] * (len(arrays) - far),
         out_specs=[pl.BlockSpec(memory_space=pltpu.VMEM)] * len(outs),
         out_shape=[jax.ShapeDtypeStruct(shape, kind) for shape, kind in outs],
-        scratch_shapes=[pltpu.VMEM(shape, kind) for shape, kind in scratch],
+        scratch_shapes=[pltpu.VMEM(shape, kind) for shape, kind in scratch]
+        + ([pltpu.SemaphoreType.DMA((sems,))] if sems else []),
         compiler_params=pltpu.CompilerParams(vmem_limit_bytes=limit << 20),
         cost_estimate=pl.CostEstimate(flops=flops, transcendentals=0, bytes_accessed=0),
     )(table, *arrays)
@@ -284,18 +286,21 @@
 
 
 def gate_up_kernel(table_ref, near_ref, far_ref, *refs):
-    *x_refs, out_ref, sums = refs
+    *x_refs, out_ref, sums, w_buf, sems = refs
     side, _, _, depth = near_ref.shape
+    for at, ref in enumerate((near_ref, far_ref)):
+        for j in range(side):
+            place = at * side + j
+            pltpu.make_async_copy(ref.at[j], w_buf.at[place], sems.at[place]).start()
     sums[...] = jnp.zeros_like(sums)
-    for at, w_ref in enumerate((near_ref, far_ref)):
-
-        @pl.loop(0, side)
-        def _(j, at=at, w_ref=w_ref):
-            place = table_ref[WEIGHTS, at * side + j]
-            cols = pl.ds(pl.multiple_of(place * depth, depth), depth)
-            x = jnp.concatenate([ref[:, cols] for ref in x_refs], axis=0)
-            sums[0] += dot(w_ref[j, 0], x, 1, 1)
-            sums[1] += dot(w_ref[j, 1], x, 1, 1)
+
+    @pl.loop(0, 2 * side)
+    def _(j):
+        cols = pl.ds(pl.multiple_of(table_ref[WEIGHTS, j] * depth, depth), depth)
+        x = jnp.concatenate([ref[:, cols] for ref in x_refs], axis=0)
+        pltpu.make_async_copy(w_buf.at[j], w_buf.at[j], sems.at[j]).wait()
+        sums[0] += dot(w_buf[j, 0], x, 1, 1)
+        sums[1] += dot(w_buf[j, 1], x, 1, 1)
 
     gate = sums[0]
     out_ref[...] = (gate / (1.0 + jnp.exp(-gate)) * sums[1]).T.astype(BF16)
@@ -310,7 +315,9 @@
         [*weights, *blocks],
         [((count, hidden), BF16)],
         8 * count * side * hidden * depth,
-        scratch=[((2, hidden, count), F32)],
+        scratch=[((2, hidden, count), F32), ((2 * side, 2, hidden, depth), BF16)],
+        far=2,
+        sems=2 * side,
     )
     return out
 
@@ -333,10 +340,7 @@
     side, _, width = weights[0].shape
     shape = (rows.shape[0] // lanes, side * width * len(weights))
     return run(
-        functools.partial(down_kernel, lanes),
-        table,
-        [rows, *weights],
-        [(shape, BF16)] * lanes,
+        functools.partial(down_kernel, lanes), table, [rows, *weights], [(shape, BF16)] * lanes
     )
 
 
@@ -391,16 +395,16 @@
     q, k, v = qkv_last(table, first, [f3, b3, f4], gain_attn, w_qkv)
 
     q = lax.all_gather(q, "c", axis=0, tiled=True)
-    queries = gathered_turned(q, "x")
+    q_far = shifted(q, "x", 2)
+    queries = [q, shifted(q, "x", 1), q_far, shifted(q, "x", 3)]
     parts = list(attend(table, (0,), queries[:1], k, v, cache))
-    for slots in ((1, 3), (2,)):
+    for slots in ((2,), (1, 3)):
         done = attend(table, slots, [queries[s] for s in slots], k, v, cache)
         parts += [shifted(part, "x", -s) for s, part in zip(slots, done)]
     mine, other = merge(table, parts)
     other = shifted(other, "c", 1)
     attended = combine(table, mine, other, lanes)
 
-    attended, gates = tied((attended, gates))
     gates = jnp.stack(gates)
     gates = [gates, shifted(gates, "c", 1)]
     heads_here = exchanged(attended, "y")

time: 257 us -> 243 us (0.946)
  waiting for transfers between devices: 122 us -> 109 us
  starting transfers between devices: 65.7 us -> 73.1 us
  local copies, waits for them, and re-layouts: 5.66 us -> 0.66 us
  blocking collectives: 25.2 us -> 20.7 us
    ppermute x41, waiting for transfers between devices: 109 us -> 92.9 us  [shifted(): lax.ppermute(value, axis, [(i, (i + step) % count) for i in range(count)])]
    ppermute x41, starting transfers between devices: 56.3 us -> 63.7 us  [shifted(): lax.ppermute(value, axis, [(i, (i + step) % count) for i in range(count)])]
    all_to_all x1, blocking collectives: 23.3 us -> 18.8 us  [exchanged(): return lax.all_to_all(value, axis, split_axis=0, concat_axis=0, tiled=True)]
    unnamed x16, local copies, waits for them, and re-layouts: 4.25 us -> 0.03 us
    all_to_all x2, waiting for transfers between devices: 12.9 us -> 16 us  [exchanged(): return lax.all_to_all(value, axis, split_axis=0, concat_axis=0, tiled=True)]
  transfers between devices with their start and end apart: 43 -> 43, of which waited for: 26 -> 25; matrix products, arithmetic and copies ran while one was open for 2% -> 2% of each run, Pallas kernels for 10% -> 11%
where the time goes in v2:
time: 243 us; the launch traced here: 241 us
  waiting for transfers between devices  109 us (45%)
  starting transfers between devices  73.1 us (30%)
  Pallas kernels  31.4 us (13%)
  blocking collectives  20.7 us (9%)
  other arithmetic  5.94 us (2%)
    ppermute x41, waiting for transfers between devices, shifted(): lax.ppermute(value, axis, [(i, (i + step) % count) for i in range(count)])  92.9 us
    ppermute x41, starting transfers between devices, shifted(): lax.ppermute(value, axis, [(i, (i + step) % count) for i in range(count)])  63.7 us
    pallas_call x12, Pallas kernels, run(): pl.pallas_call(kernel, in_specs=[pl.BlockSpec(memory_space=pltpu.SMEM)] +...  31.4 us
    all_to_all x1, blocking collectives, exchanged(): return lax.all_to_all(value, axis, split_axis=0, concat_axis=0, tiled=True)  18.8 us
    all_to_all x2, waiting for transfers between devices, exchanged(): return lax.all_to_all(value, axis, split_axis=0, concat_axis=0, tiled=True)  16 us
    all_to_all x2, starting transfers between devices, exchanged(): return lax.all_to_all(value, axis, split_axis=0, concat_axis=0, tiled=True)  9.37 us
  transfers between devices with their start and end apart: 43, of which 25 were waited for; matrix products, arithmetic and copies ran while one was open for 2% of the time, Pallas kernels for 11%

profile of v2, /device:TPU:2, one launch (start us, length us, event | category | flops | bytes accessed | tf_op | source)
XLA Modules:
  0.0 241.0 jit_solution(8595716886108436378)
XLA Ops:
  0.0 2.2 collective-permute-start.22
  4.8 3.0 %collective-permute-start.2 = (bf16[8,4096]{1,0:T(8,128)(2,1)}, bf16[8,4096]{1,0:T(8,128)(2,1)S(1)}, u32[]{:S(2)}, u32[]{:S(2)}) collective-permute-start(bf16[8,4096]{1,0:T(8,128)(2,1)} %hidden_ref.1), channel_id=1, source_target_pairs={{0,24},{8,0},{16,8},{24,16},{1,25},{9,1},{17,9},{25,17},{2,26},{10... | collective-permute-start | bytes 196616 | tf_op jit(solution)/shard_map/ppermute | solution.py:26
  11.3 2.7 %collective-permute-done.1 = bf16[8,4096]{1,0:T(8,128)(2,1)S(1)} collective-permute-done((bf16[8,4096]{1,0:T(8,128)(2,1)}, bf16[8,4096]{1,0:T(8,128)(2,1)S(1)}, u32[]{:S(2)}, u32[]{:S(2)}) %collective-permute-start.1) | collective-permute-done | bytes 65568 | tf_op jit(solution)/shard_map/ppermute | solution.py:26
  14.0 2.0 collective-permute-done
  16.8 2.0 collective-permute-start.3
  18.8 4.0 %collective-permute-start.4 = (bf16[32,4096]{1,0:T(8,128)(2,1)S(1)}, bf16[32,4096]{1,0:T(8,128)(2,1)}, u32[]{:S(2)}, u32[]{:S(2)}) collective-permute-start(bf16[32,4096]{1,0:T(8,128)(2,1)S(1)} %pad_maximum_fusion.2.refs_0_), channel_id=1, source_target_pairs={{0,224},{32,0},{64,32},{96,64},{128,96},{160,128},{192,160},{224,1... | collective-permute-start | bytes 786440 | tf_op jit(solution)/shard_map/ppermute | solution.py:26
  22.8 11.0 %collective-permute-done.21 = bf16[2,344,512]{2,1,0:T(8,128)(2,1)S(1)} collective-permute-done((bf16[2,344,512]{2,1,0:T(8,128)(2,1)}, bf16[2,344,512]{2,1,0:T(8,128)(2,1)S(1)}, u32[]{:S(2)}, u32[]{:S(2)}) %collective-permute-start.21) | collective-permute-done | bytes 704544 | tf_op jit(solution)/shard_map/ppermute | solution.py:26
  34.7 2.9 %pad_maximum_fusion.near_ref = bf16[4,2,344,512]{3,2,1,0:T(8,128)(2,1)} fusion(bf16[1,2,344,512]{3,2,1,0:T(8,128)(2,1)S(1)} %bitcast.28, bf16[1,2,344,512]{3,2,1,0:T(8,128)(2,1)S(1)} %bitcast.29, bf16[1,2,344,512]{3,2,1,0:T(8,128)(2,1)S(1)} %bitcast.30, bf16[1,2,344,512]{3,2,1,0:T(8,128)(2,1)} %bitcast.27), kind=kLoop, calls=%fused_computation | loop fusion | flops 4227072 | bytes 5636096 | tf_op jit(solution)/shard_map/stack | solution.py:408
  37.5 2.0 collective-permute-start.5
  39.5 4.0 %collective-permute-start.6 = (bf16[32,4096]{1,0:T(8,128)(2,1)}, bf16[32,4096]{1,0:T(8,128)(2,1)}, u32[]{:S(2)}, u32[]{:S(2)}) collective-permute-start(bf16[32,4096]{1,0:T(8,128)(2,1)} %collective-permute-done.4.refs_2_), channel_id=1, source_target_pairs={{0,224},{32,0},{64,32},{96,64},{128,96},{160,128},{192,160},{224,1... | collective-permute-start | bytes 786440 | tf_op jit(solution)/shard_map/ppermute | solution.py:26
  43.6 7.1 %collective-permute-done.5.refs_3_ = bf16[32,4096]{1,0:T(8,128)(2,1)} collective-permute-done((bf16[32,4096]{1,0:T(8,128)(2,1)}, bf16[32,4096]{1,0:T(8,128)(2,1)}, u32[]{:S(2)}, u32[]{:S(2)}) %collective-permute-start.5) | collective-permute-done | bytes 262176 | tf_op jit(solution)/shard_map/ppermute | solution.py:26
  51.3 3.2 %collective-permute-start.8 = (bf16[32,4096]{1,0:T(8,128)(2,1)}, bf16[32,4096]{1,0:T(8,128)(2,1)}, u32[]{:S(2)}, u32[]{:S(2)}) collective-permute-start(bf16[32,4096]{1,0:T(8,128)(2,1)} %collective-permute-done.6.refs_4_), channel_id=1, source_target_pairs={{0,224},{32,0},{64,32},{96,64},{128,96},{160,128},{192,160},{224,1... | collective-permute-start | bytes 786440 | tf_op jit(solution)/shard_map/ppermute | solution.py:26
  54.6 5.7 %collective-permute-done.7.refs_0_ = bf16[32,4096]{1,0:T(8,128)(2,1)} collective-permute-done((bf16[32,4096]{1,0:T(8,128)(2,1)}, bf16[32,4096]{1,0:T(8,128)(2,1)}, u32[]{:S(2)}, u32[]{:S(2)}) %collective-permute-start.7) | collective-permute-done | bytes 262176 | tf_op jit(solution)/shard_map/ppermute | solution.py:26
  61.6 3.1 %collective-permute-start.17 = (bf16[128,4096]{1,0:T(8,128)(2,1)}, bf16[128,4096]{1,0:T(8,128)(2,1)}, u32[]{:S(2)}, u32[]{:S(2)}) collective-permute-start(bf16[128,4096]{1,0:T(8,128)(2,1)} %refs_0_), channel_id=1, source_target_pairs={{0,24},{8,0},{16,8},{24,16},{1,25},{9,1},{17,9},{25,17},{2,26},{10... | collective-permute-start | bytes 3145736 | tf_op jit(solution)/shard_map/ppermute | solution.py:26
  66.3 3.1 %shard_map.91.first_ref = bf16[160,384]{1,0:T(8,128)(2,1)S(1)} custom-call(s32[8,8]{1,0:T(8,128)S(1)} %stack.41.table_ref, f32[1,4096]{1,0:T(1,128)S(1)} %bitcast.21, bf16[4096,384]{1,0:T(8,128)(2,1)S(1)} %bitcast.16, bf16[32,4096]{1,0:T(8,128)(2,1)S(1)} %pad_maximum_fusion.2.refs_0_, bf16[32,4096]{1,0:T(8,128)(2,1)} %collective-permute-done.3.refs_1_, ...), custom_call_target="tpu_custom_call" | custom-call | flops 503316480 | tf_op jit(solution)/shard_map/pallas_call | solution.py:38
  69.4 2.8 %shard_map.92 = (bf16[256,128]{1,0:T(8,128)(2,1)S(1)}, bf16[256,128]{1,0:T(8,128)(2,1)S(1)}, bf16[256,128]{1,0:T(8,128)(2,1)S(1)}) custom-call(s32[8,8]{1,0:T(8,128)S(1)} %stack.41.table_ref, f32[1,4096]{1,0:T(1,128)S(1)} %bitcast.22, bf16[4096,384]{1,0:T(8,128)(2,1)S(1)} %bitcast.17, bf16[160,384]{1,0:T(8,128)(2,1)S(1)} %shard_map.91.first_ref, ...), custom_call_target="tpu_custom_call" | custom-call | flops 301989888 | tf_op jit(solution)/shard_map/pallas_call | solution.py:38
  72.2 1.9 all_gather.3.refs_0_
  74.1 2.1 collective-permute-start.10
  76.3 4.9 %collective-permute-done.10.refs_0_ = bf16[512,128]{1,0:T(8,128)(2,1)S(1)} collective-permute-done((bf16[512,128]{1,0:T(8,128)(2,1)S(1)}, bf16[512,128]{1,0:T(8,128)(2,1)S(1)}, u32[]{:S(2)}, u32[]{:S(2)}) %collective-permute-start.10) | collective-permute-done | bytes 131104 | tf_op jit(solution)/shard_map/ppermute | solution.py:26
  82.6 4.3 %collective-permute-done.12.refs_0_ = bf16[512,128]{1,0:T(8,128)(2,1)S(1)} collective-permute-done((bf16[512,128]{1,0:T(8,128)(2,1)S(1)}, bf16[512,128]{1,0:T(8,128)(2,1)S(1)}, u32[]{:S(2)}, u32[]{:S(2)}) %collective-permute-start.12) | collective-permute-done | bytes 131104 | tf_op jit(solution)/shard_map/ppermute | solution.py:26
  86.9 3.1 %collective-permute-start.13 = (bf16[512,128]{1,0:T(8,128)(2,1)S(1)}, bf16[512,128]{1,0:T(8,128)(2,1)S(1)}, u32[]{:S(2)}, u32[]{:S(2)}) collective-permute-start(bf16[512,128]{1,0:T(8,128)(2,1)S(1)} %all_gather.3.refs_0_), channel_id=1, source_target_pairs={{0,6},{2,0},{4,2},{6,4},{1,7},{3,1},{5,3},{7,5},{8,14},{10,8},{12,... | collective-permute-start | bytes 393224 | tf_op jit(solution)/shard_map/ppermute | solution.py:26
  90.1 2.6 %shard_map.94 = bf16[144,512]{1,0:T(8,128)(2,1)S(1)} custom-call(s32[8,8]{1,0:T(8,128)S(1)} %stack.41.table_ref, bf16[256,128]{1,0:T(8,128)(2,1)S(1)} %get-tuple-element.25.k_ref, bf16[256,128]{1,0:T(8,128)(2,1)S(1)} %get-tuple-element.26.v_ref, bf16[2,1024,256]{2,1,0:T(8,128)(2,1)S(1)} %bitcast.18, bf16[512,128]{1,0:T(8,128)(2,1)S(1)} %collective-permute-done.10.refs_0_), custom_call_target="tpu_custom_call" | custom-call | flops 335544320 | tf_op jit(solution)/shard_map/pallas_call | solution.py:38
  92.7 2.4 collective-permute-start.11
  95.1 4.5 %shard_map.95 = (bf16[144,512]{1,0:T(8,128)(2,1)S(1)}, bf16[144,512]{1,0:T(8,128)(2,1)S(1)}) custom-call(s32[8,8]{1,0:T(8,128)S(1)} %stack.41.table_ref, bf16[256,128]{1,0:T(8,128)(2,1)S(1)} %get-tuple-element.25.k_ref, bf16[256,128]{1,0:T(8,128)(2,1)S(1)} %get-tuple-element.26.v_ref, bf16[2,1024,256]{2,1,0:T(8,128)(2,1)S(1)} %bitcast.19, ...), custom_call_target="tpu_custom_call" | custom-call | flops 671088640 | tf_op jit(solution)/shard_map/pallas_call | solution.py:38
  99.6 2.1 collective-permute-start.14
  101.7 3.2 %collective-permute-done.14.refs_2_ = bf16[144,512]{1,0:T(8,128)(2,1)S(1)} collective-permute-done((bf16[144,512]{1,0:T(8,128)(2,1)S(1)}, bf16[144,512]{1,0:T(8,128)(2,1)S(1)}, u32[]{:S(2)}, u32[]{:S(2)}) %collective-permute-start.14) | collective-permute-done | bytes 147488 | tf_op jit(solution)/shard_map/ppermute | solution.py:26
  106.2 2.6 %shard_map.93.refs_0_ = bf16[144,512]{1,0:T(8,128)(2,1)S(1)} custom-call(s32[8,8]{1,0:T(8,128)S(1)} %stack.41.table_ref, bf16[256,128]{1,0:T(8,128)(2,1)S(1)} %get-tuple-element.25.k_ref, bf16[256,128]{1,0:T(8,128)(2,1)S(1)} %get-tuple-element.26.v_ref, bf16[2,1024,256]{2,1,0:T(8,128)(2,1)S(1)} %bitcast.20, bf16[512,128]{1,0:T(8,128)(2,1)S(1)} %all_gather.3.refs_0_), custom_call_target="tpu_custom_call" | custom-call | flops 335544320 | tf_op jit(solution)/shard_map/pallas_call | solution.py:38
  113.4 4.0 %all-to-all-start = ((bf16[4,64,128]{2,1,0:T(8,128)(2,1)}), bf16[4,64,128]{2,1,0:T(8,128)(2,1)S(1)}, u32[]{:S(2)}, u32[]{:S(2)}) async-start(bf16[4,64,128]{2,1,0:T(8,128)(2,1)} %shard_map.97), calls=%async_computation | async-start | bytes 131072 | tf_op jit(solution)/shard_map/all_to_all | solution.py:384
  117.5 5.6 %all-to-all-done.heads_ref = bf16[4,64,128]{2,1,0:T(8,128)(2,1)S(1)} async-done(((bf16[4,64,128]{2,1,0:T(8,128)(2,1)}), bf16[4,64,128]{2,1,0:T(8,128)(2,1)S(1)}, u32[]{:S(2)}, u32[]{:S(2)}) %all-to-all-start) | async-done | bytes 65568 | tf_op jit(solution)/shard_map/all_to_all | solution.py:384
  123.0 3.9 %shard_map.98 = bf16[8,8,4096]{2,1,0:T(8,128)(2,1)} custom-call(s32[8,8]{1,0:T(8,128)S(1)} %stack.41.table_ref, bf16[4,64,128]{2,1,0:T(8,128)(2,1)S(1)} %all-to-all-done.heads_ref, bf16[128,4096]{1,0:T(8,128)(2,1)S(1)} %copy-done.2, bf16[128,4096]{1,0:T(8,128)(2,1)} %collective-permute-done.17.refs_1_, bf16[128,4096]{1,0:T(8,128)(2,1)} %collective-permute-done.18.refs_2_, ...), custom_call_target="tpu_custom_call" | custom-call | tf_op jit(solution)/shard_map/pallas_call | solution.py:38
  126.9 5.4 %all-to-all-start.1 = ((bf16[8,8,4096]{2,1,0:T(8,128)(2,1)}), bf16[8,8,4096]{2,1,0:T(8,128)(2,1)S(1)}, u32[]{:S(2)}, u32[]{:S(2)}) async-start(bf16[8,8,4096]{2,1,0:T(8,128)(2,1)} %shard_map.98), calls=%async_computation.1 | async-start | bytes 1048576 | tf_op jit(solution)/shard_map/all_to_all | solution.py:384
  132.3 3.3 %collective-permute-start.36 = (bf16[344,512]{1,0:T(8,128)(2,1)S(1)}, bf16[344,512]{1,0:T(8,128)(2,1)S(1)}, u32[]{:S(2)}, u32[]{:S(2)}) collective-permute-start(bf16[344,512]{1,0:T(8,128)(2,1)S(1)} %copy-done.6), channel_id=1, source_target_pairs={{0,6},{2,0},{4,2},{6,4},{1,7},{3,1},{5,3},{7,5},{8,14},{10,8},{12,... | collective-permute-start | bytes 1056776 | tf_op jit(solution)/shard_map/ppermute | solution.py:26
  135.7 2.5 %collective-permute-start.34 = (bf16[344,512]{1,0:T(8,128)(2,1)S(1)}, bf16[344,512]{1,0:T(8,128)(2,1)S(1)}, u32[]{:S(2)}, u32[]{:S(2)}) collective-permute-start(bf16[344,512]{1,0:T(8,128)(2,1)S(1)} %copy-done.6), channel_id=1, source_target_pairs={{0,2},{2,4},{4,6},{6,0},{1,3},{3,5},{5,7},{7,1},{8,10},{10,12},{12... | collective-permute-start | bytes 1056776 | tf_op jit(solution)/shard_map/ppermute | solution.py:26
  138.3 10.4 %all-to-all-done.1.terms_ref = bf16[8,8,4096]{2,1,0:T(8,128)(2,1)S(1)} async-done(((bf16[8,8,4096]{2,1,0:T(8,128)(2,1)}), bf16[8,8,4096]{2,1,0:T(8,128)(2,1)S(1)}, u32[]{:S(2)}, u32[]{:S(2)}) %all-to-all-start.1) | async-done | bytes 524320 | tf_op jit(solution)/shard_map/all_to_all | solution.py:384
  153.9 2.8 %collective-permute-done.25 = bf16[8,4096]{1,0:T(8,128)(2,1)S(1)} collective-permute-done((bf16[8,4096]{1,0:T(8,128)(2,1)S(1)}, bf16[8,4096]{1,0:T(8,128)(2,1)S(1)}, u32[]{:S(2)}, u32[]{:S(2)}) %collective-permute-start.25) | collective-permute-done | bytes 65568 | tf_op jit(solution)/shard_map/ppermute | solution.py:26
  158.4 2.7 %collective-permute-start.28 = (bf16[32,4096]{1,0:T(8,128)(2,1)S(1)}, bf16[32,4096]{1,0:T(8,128)(2,1)S(1)}, u32[]{:S(2)}, u32[]{:S(2)}) collective-permute-start(bf16[32,4096]{1,0:T(8,128)(2,1)S(1)} %pad_maximum_fusion.3.refs_0_), channel_id=1, source_target_pairs={{0,224},{32,0},{64,32},{96,64},{128,96},{160,128},{192,160},{224,1... | collective-permute-start | bytes 786440 | tf_op jit(solution)/shard_map/ppermute | solution.py:26
  161.1 5.4 %collective-permute-done.27.refs_1_ = bf16[32,4096]{1,0:T(8,128)(2,1)S(1)} collective-permute-done((bf16[32,4096]{1,0:T(8,128)(2,1)S(1)}, bf16[32,4096]{1,0:T(8,128)(2,1)S(1)}, u32[]{:S(2)}, u32[]{:S(2)}) %collective-permute-start.27) | collective-permute-done | bytes 262176 | tf_op jit(solution)/shard_map/ppermute | solution.py:26
  166.5 3.5 %collective-permute-start.30 = (bf16[32,4096]{1,0:T(8,128)(2,1)S(1)}, bf16[32,4096]{1,0:T(8,128)(2,1)S(1)}, u32[]{:S(2)}, u32[]{:S(2)}) collective-permute-start(bf16[32,4096]{1,0:T(8,128)(2,1)S(1)} %collective-permute-done.28.refs_2_), channel_id=1, source_target_pairs={{0,224},{32,0},{64,32},{96,64},{128,96},{160,128},{192,160},{224,1... | collective-permute-start | bytes 786440 | tf_op jit(solution)/shard_map/ppermute | solution.py:26
  170.0 6.3 %collective-permute-done.29.refs_3_ = bf16[32,4096]{1,0:T(8,128)(2,1)S(1)} collective-permute-done((bf16[32,4096]{1,0:T(8,128)(2,1)S(1)}, bf16[32,4096]{1,0:T(8,128)(2,1)S(1)}, u32[]{:S(2)}, u32[]{:S(2)}) %collective-permute-start.29) | collective-permute-done | bytes 262176 | tf_op jit(solution)/shard_map/ppermute | solution.py:26
  176.4 3.7 %collective-permute-start.32 = (bf16[32,4096]{1,0:T(8,128)(2,1)S(1)}, bf16[32,4096]{1,0:T(8,128)(2,1)S(1)}, u32[]{:S(2)}, u32[]{:S(2)}) collective-permute-start(bf16[32,4096]{1,0:T(8,128)(2,1)S(1)} %collective-permute-done.30.refs_4_), channel_id=1, source_target_pairs={{0,224},{32,0},{64,32},{96,64},{128,96},{160,128},{192,160},{224,1... | collective-permute-start | bytes 786440 | tf_op jit(solution)/shard_map/ppermute | solution.py:26
  180.1 6.0 %collective-permute-done.31.refs_5_ = bf16[32,4096]{1,0:T(8,128)(2,1)S(1)} collective-permute-done((bf16[32,4096]{1,0:T(8,128)(2,1)S(1)}, bf16[32,4096]{1,0:T(8,128)(2,1)S(1)}, u32[]{:S(2)}, u32[]{:S(2)}) %collective-permute-start.31) | collective-permute-done | bytes 262176 | tf_op jit(solution)/shard_map/ppermute | solution.py:26
  186.1 7.6 %collective-permute-done.33.refs_7_ = bf16[32,4096]{1,0:T(8,128)(2,1)S(1)} collective-permute-done((bf16[32,4096]{1,0:T(8,128)(2,1)S(1)}, bf16[32,4096]{1,0:T(8,128)(2,1)S(1)}, u32[]{:S(2)}, u32[]{:S(2)}) %collective-permute-start.33) | collective-permute-done | bytes 262176 | tf_op jit(solution)/shard_map/ppermute | solution.py:26
  193.7 5.1 %shard_map.100.x_ref = bf16[256,344]{1,0:T(8,128)(2,1)S(1)} custom-call(s32[8,8]{1,0:T(8,128)S(1)} %stack.41.table_ref, bf16[4,2,344,512]{3,2,1,0:T(8,128)(2,1)} %pad_maximum_fusion.near_ref, bf16[4,2,344,512]{3,2,1,0:T(8,128)(2,1)} %collective-permute-done.23.far_ref, bf16[32,4096]{1,0:T(8,128)(2,1)S(1)} %pad_maximum_fusion.3.refs_0_, ...), custom_call_target="tpu_custom_call" | custom-call | flops 1442840576 | tf_op jit(solution)/shard_map/pallas_call | solution.py:38
  198.9 3.0 %shard_map.101 = (bf16[64,4096]{1,0:T(8,128)(2,1)S(1)}, bf16[64,4096]{1,0:T(8,128)(2,1)S(1)}, bf16[64,4096]{1,0:T(8,128)(2,1)S(1)}, bf16[64,4096]{1,0:T(8,128)(2,1)S(1)}) custom-call(s32[8,8]{1,0:T(8,128)S(1)} %stack.41.table_ref, bf16[256,344]{1,0:T(8,128)(2,1)S(1)} %shard_map.100.x_ref, bf16[4,344,512]{2,1,0:T(8,128)(2,1)S(1)} %pad_maximum_fusion.1.refs_0_, ...), custom_call_target="tpu_custom_call" | custom-call | tf_op jit(solution)/shard_map/pallas_call | solution.py:38
  202.1 1.9 collective-permute-start.40
  204.0 9.4 %collective-permute-done.38.refs_1_ = bf16[64,4096]{1,0:T(8,128)(2,1)S(1)} collective-permute-done((bf16[64,4096]{1,0:T(8,128)(2,1)S(1)}, bf16[64,4096]{1,0:T(8,128)(2,1)S(1)}, u32[]{:S(2)}, u32[]{:S(2)}) %collective-permute-start.38) | collective-permute-done | bytes 524320 | tf_op jit(solution)/shard_map/ppermute | solution.py:26
  215.1 5.5 %collective-permute-done.40.refs_3_ = bf16[64,4096]{1,0:T(8,128)(2,1)S(1)} collective-permute-done((bf16[64,4096]{1,0:T(8,128)(2,1)S(1)}, bf16[64,4096]{1,0:T(8,128)(2,1)S(1)}, u32[]{:S(2)}, u32[]{:S(2)}) %collective-permute-start.40) | collective-permute-done | bytes 524320 | tf_op jit(solution)/shard_map/ppermute | solution.py:26
  221.5 18.8 %all_to_all.15 = bf16[8,8,4096]{2,1,0:T(8,128)(2,1)S(1)} all-to-all(bf16[8,8,4096]{2,1,0:T(8,128)(2,1)S(1)} %shard_map.102), channel_id=1, replica_groups=mesh['z'=8,'y'=4,'x'=4,'c'=2] {'z'}, dimensions={0} | all-to-all | bytes 1048576 | tf_op jit(solution)/shard_map/all_to_all | solution.py:384
  (81 shorter events, 29.4 us)
Async XLA Ops:
  0.0 22.8 %collective-permute-start.22 = (bf16[2,344,512]{2,1,0:T(8,128)(2,1)}, bf16[2,344,512]{2,1,0:T(8,128)(2,1)S(1)}, u32[]{:S(2)}, u32[]{:S(2)}) collective-permute-start(bf16[2,344,512]{2,1,0:T(8,128)(2,1)} %bitcast.24), channel_id=1, source_target_pairs={{0,6},{2,0},{4,2},{6,4},{1,7},{3,1},{5,3},{7,5},{8,14},{10,8},{12,... | collective-permute-start | bytes 2113544 | tf_op jit(solution)/shard_map/ppermute | solution.py:26
  2.2 31.5 %collective-permute-start.21 = (bf16[2,344,512]{2,1,0:T(8,128)(2,1)}, bf16[2,344,512]{2,1,0:T(8,128)(2,1)S(1)}, u32[]{:S(2)}, u32[]{:S(2)}) collective-permute-start(bf16[2,344,512]{2,1,0:T(8,128)(2,1)} %bitcast.25), channel_id=1, source_target_pairs={{0,4},{2,6},{4,0},{6,2},{1,5},{3,7},{5,1},{7,3},{8,12},{10,14},{12... | collective-permute-start | bytes 2113544 | tf_op jit(solution)/shard_map/ppermute | solution.py:26
  3.0 31.7 %collective-permute-start.20 = (bf16[2,344,512]{2,1,0:T(8,128)(2,1)}, bf16[2,344,512]{2,1,0:T(8,128)(2,1)S(1)}, u32[]{:S(2)}, u32[]{:S(2)}) collective-permute-start(bf16[2,344,512]{2,1,0:T(8,128)(2,1)} %bitcast.26), channel_id=1, source_target_pairs={{0,2},{2,4},{4,6},{6,0},{1,3},{3,5},{5,7},{7,1},{8,10},{10,12},{12... | collective-permute-start | bytes 2113544 | tf_op jit(solution)/shard_map/ppermute | solution.py:26
  4.8 5.2 %collective-permute-start.2 = (bf16[8,4096]{1,0:T(8,128)(2,1)}, bf16[8,4096]{1,0:T(8,128)(2,1)S(1)}, u32[]{:S(2)}, u32[]{:S(2)}) collective-permute-start(bf16[8,4096]{1,0:T(8,128)(2,1)} %hidden_ref.1), channel_id=1, source_target_pairs={{0,24},{8,0},{16,8},{24,16},{1,25},{9,1},{17,9},{25,17},{2,26},{10... | collective-permute-start | bytes 196616 | tf_op jit(solution)/shard_map/ppermute | solution.py:26
  7.8 6.2 %collective-permute-start.1 = (bf16[8,4096]{1,0:T(8,128)(2,1)}, bf16[8,4096]{1,0:T(8,128)(2,1)S(1)}, u32[]{:S(2)}, u32[]{:S(2)}) collective-permute-start(bf16[8,4096]{1,0:T(8,128)(2,1)} %hidden_ref.1), channel_id=1, source_target_pairs={{0,16},{8,24},{16,0},{24,8},{1,17},{9,25},{17,1},{25,9},{2,18},{10... | collective-permute-start | bytes 196616 | tf_op jit(solution)/shard_map/ppermute | solution.py:26
  10.0 5.9 %collective-permute-start = (bf16[8,4096]{1,0:T(8,128)(2,1)}, bf16[8,4096]{1,0:T(8,128)(2,1)S(1)}, u32[]{:S(2)}, u32[]{:S(2)}) collective-permute-start(bf16[8,4096]{1,0:T(8,128)(2,1)} %hidden_ref.1), channel_id=1, source_target_pairs={{0,8},{8,16},{16,24},{24,0},{1,9},{9,17},{17,25},{25,1},{2,10},{10... | collective-permute-start | bytes 196616 | tf_op jit(solution)/shard_map/ppermute | solution.py:26
  16.8 20.8 %collective-permute-start.3 = (bf16[32,4096]{1,0:T(8,128)(2,1)S(1)}, bf16[32,4096]{1,0:T(8,128)(2,1)}, u32[]{:S(2)}, u32[]{:S(2)}) collective-permute-start(bf16[32,4096]{1,0:T(8,128)(2,1)S(1)} %pad_maximum_fusion.2.refs_0_), channel_id=1, source_target_pairs={{0,32},{32,64},{64,96},{96,128},{128,160},{160,192},{192,224},{224... | collective-permute-start | bytes 786440 | tf_op jit(solution)/shard_map/ppermute | solution.py:26
  18.8 20.8 %collective-permute-start.4 = (bf16[32,4096]{1,0:T(8,128)(2,1)S(1)}, bf16[32,4096]{1,0:T(8,128)(2,1)}, u32[]{:S(2)}, u32[]{:S(2)}) collective-permute-start(bf16[32,4096]{1,0:T(8,128)(2,1)S(1)} %pad_maximum_fusion.2.refs_0_), channel_id=1, source_target_pairs={{0,224},{32,0},{64,32},{96,64},{128,96},{160,128},{192,160},{224,1... | collective-permute-start | bytes 786440 | tf_op jit(solution)/shard_map/ppermute | solution.py:26
  34.7 31.7 %copy-start = (bf16[4096,1,384]{2,0,1:T(8,128)(2,1)S(1)}, bf16[4096,1,384]{2,0,1:T(8,128)(2,1)}, u32[]{:S(2)}) copy-start(bf16[4096,1,384]{2,0,1:T(8,128)(2,1)} %param.11) | copy-start | bytes 9437188
  34.7 31.7 %copy-start.4 = (f32[4096]{0:T(1024)S(1)}, f32[4096]{0:T(1024)}, u32[]{:S(2)}) copy-start(f32[4096]{0:T(1024)} %param.10) | copy-start | bytes 49156
  37.5 112.0 %collective-permute-start.23 = (bf16[4,2,344,512]{3,2,1,0:T(8,128)(2,1)}, bf16[4,2,344,512]{3,2,1,0:T(8,128)(2,1)}, u32[]{:S(2)}, u32[]{:S(2)}) collective-permute-start(bf16[4,2,344,512]{3,2,1,0:T(8,128)(2,1)} %pad_maximum_fusion.near_ref), channel_id=1, source_target_pairs={{0,1},{1,0},{2,3},{3,2},{4,5},{5,4},{6,7},{7,6},{8,9},{9,8},{10,11... | collective-permute-start | bytes 8454152 | tf_op jit(solution)/shard_map/ppermute | solution.py:26
  37.5 13.1 %collective-permute-start.5 = (bf16[32,4096]{1,0:T(8,128)(2,1)}, bf16[32,4096]{1,0:T(8,128)(2,1)}, u32[]{:S(2)}, u32[]{:S(2)}) collective-permute-start(bf16[32,4096]{1,0:T(8,128)(2,1)} %collective-permute-done.3.refs_1_), channel_id=1, source_target_pairs={{0,32},{32,64},{64,96},{96,128},{128,160},{160,192},{192,224},{224... | collective-permute-start | bytes 786440 | tf_op jit(solution)/shard_map/ppermute | solution.py:26
  39.5 11.8 %collective-permute-start.6 = (bf16[32,4096]{1,0:T(8,128)(2,1)}, bf16[32,4096]{1,0:T(8,128)(2,1)}, u32[]{:S(2)}, u32[]{:S(2)}) collective-permute-start(bf16[32,4096]{1,0:T(8,128)(2,1)} %collective-permute-done.4.refs_2_), channel_id=1, source_target_pairs={{0,224},{32,0},{64,32},{96,64},{128,96},{160,128},{192,160},{224,1... | collective-permute-start | bytes 786440 | tf_op jit(solution)/shard_map/ppermute | solution.py:26
  50.7 9.6 %collective-permute-start.7 = (bf16[32,4096]{1,0:T(8,128)(2,1)}, bf16[32,4096]{1,0:T(8,128)(2,1)}, u32[]{:S(2)}, u32[]{:S(2)}) collective-permute-start(bf16[32,4096]{1,0:T(8,128)(2,1)} %collective-permute-done.5.refs_3_), channel_id=1, source_target_pairs={{0,32},{32,64},{64,96},{96,128},{128,160},{160,192},{192,224},{224... | collective-permute-start | bytes 786440 | tf_op jit(solution)/shard_map/ppermute | solution.py:26
  51.3 14.1 %collective-permute-start.8 = (bf16[32,4096]{1,0:T(8,128)(2,1)}, bf16[32,4096]{1,0:T(8,128)(2,1)}, u32[]{:S(2)}, u32[]{:S(2)}) collective-permute-start(bf16[32,4096]{1,0:T(8,128)(2,1)} %collective-permute-done.6.refs_4_), channel_id=1, source_target_pairs={{0,224},{32,0},{64,32},{96,64},{128,96},{160,128},{192,160},{224,1... | collective-permute-start | bytes 786440 | tf_op jit(solution)/shard_map/ppermute | solution.py:26
  60.3 9.1 %collective-permute-start.9 = (bf16[32,4096]{1,0:T(8,128)(2,1)}, bf16[32,4096]{1,0:T(8,128)(2,1)}, u32[]{:S(2)}, u32[]{:S(2)}) collective-permute-start(bf16[32,4096]{1,0:T(8,128)(2,1)} %collective-permute-done.7.refs_0_), channel_id=1, source_target_pairs={{0,32},{32,64},{64,96},{96,128},{128,160},{160,192},{192,224},{224... | collective-permute-start | bytes 786440 | tf_op jit(solution)/shard_map/ppermute | solution.py:26
  61.6 55.8 %collective-permute-start.17 = (bf16[128,4096]{1,0:T(8,128)(2,1)}, bf16[128,4096]{1,0:T(8,128)(2,1)}, u32[]{:S(2)}, u32[]{:S(2)}) collective-permute-start(bf16[128,4096]{1,0:T(8,128)(2,1)} %refs_0_), channel_id=1, source_target_pairs={{0,24},{8,0},{16,8},{24,16},{1,25},{9,1},{17,9},{25,17},{2,26},{10... | collective-permute-start | bytes 3145736 | tf_op jit(solution)/shard_map/ppermute | solution.py:26
  64.7 52.7 %collective-permute-start.18 = (bf16[128,4096]{1,0:T(8,128)(2,1)}, bf16[128,4096]{1,0:T(8,128)(2,1)}, u32[]{:S(2)}, u32[]{:S(2)}) collective-permute-start(bf16[128,4096]{1,0:T(8,128)(2,1)} %refs_0_), channel_id=1, source_target_pairs={{0,16},{8,24},{16,0},{24,8},{1,17},{9,25},{17,1},{25,9},{2,18},{10... | collective-permute-start | bytes 3145736 | tf_op jit(solution)/shard_map/ppermute | solution.py:26
  65.3 52.1 %collective-permute-start.19 = (bf16[128,4096]{1,0:T(8,128)(2,1)}, bf16[128,4096]{1,0:T(8,128)(2,1)}, u32[]{:S(2)}, u32[]{:S(2)}) collective-permute-start(bf16[128,4096]{1,0:T(8,128)(2,1)} %refs_0_), channel_id=1, source_target_pairs={{0,8},{8,16},{16,24},{24,0},{1,9},{9,17},{17,25},{25,1},{2,10},{10... | collective-permute-start | bytes 3145736 | tf_op jit(solution)/shard_map/ppermute | solution.py:26
  74.1 7.1 %collective-permute-start.10 = (bf16[512,128]{1,0:T(8,128)(2,1)S(1)}, bf16[512,128]{1,0:T(8,128)(2,1)S(1)}, u32[]{:S(2)}, u32[]{:S(2)}) collective-permute-start(bf16[512,128]{1,0:T(8,128)(2,1)S(1)} %all_gather.3.refs_0_), channel_id=1, source_target_pairs={{0,4},{2,6},{4,0},{6,2},{1,5},{3,7},{5,1},{7,3},{8,12},{10,14},{12... | collective-permute-start | bytes 393224 | tf_op jit(solution)/shard_map/ppermute | solution.py:26
  81.2 5.7 %collective-permute-start.12 = (bf16[512,128]{1,0:T(8,128)(2,1)S(1)}, bf16[512,128]{1,0:T(8,128)(2,1)S(1)}, u32[]{:S(2)}, u32[]{:S(2)}) collective-permute-start(bf16[512,128]{1,0:T(8,128)(2,1)S(1)} %all_gather.3.refs_0_), channel_id=1, source_target_pairs={{0,2},{2,4},{4,6},{6,0},{1,3},{3,5},{5,7},{7,1},{8,10},{10,12},{12... | collective-permute-start | bytes 393224 | tf_op jit(solution)/shard_map/ppermute | solution.py:26
  86.9 5.7 %collective-permute-start.13 = (bf16[512,128]{1,0:T(8,128)(2,1)S(1)}, bf16[512,128]{1,0:T(8,128)(2,1)S(1)}, u32[]{:S(2)}, u32[]{:S(2)}) collective-permute-start(bf16[512,128]{1,0:T(8,128)(2,1)S(1)} %all_gather.3.refs_0_), channel_id=1, source_target_pairs={{0,6},{2,0},{4,2},{6,4},{1,7},{3,1},{5,3},{7,5},{8,14},{10,8},{12,... | collective-permute-start | bytes 393224 | tf_op jit(solution)/shard_map/ppermute | solution.py:26
  90.1 33.0 %copy-start.2 = (bf16[128,4096]{1,0:T(8,128)(2,1)S(1)}, bf16[128,4096]{1,0:T(8,128)(2,1)}, u32[]{:S(2)}) copy-start(bf16[128,4096]{1,0:T(8,128)(2,1)} %refs_0_) | copy-start | bytes 3145732
  92.7 6.9 %collective-permute-start.11 = (bf16[144,512]{1,0:T(8,128)(2,1)S(1)}, bf16[144,512]{1,0:T(8,128)(2,1)S(1)}, u32[]{:S(2)}, u32[]{:S(2)}) collective-permute-start(bf16[144,512]{1,0:T(8,128)(2,1)S(1)} %shard_map.94), channel_id=1, source_target_pairs={{0,4},{2,6},{4,0},{6,2},{1,5},{3,7},{5,1},{7,3},{8,12},{10,14},{12... | collective-permute-start | bytes 442376 | tf_op jit(solution)/shard_map/ppermute | solution.py:26
  99.6 5.2 %collective-permute-start.14 = (bf16[144,512]{1,0:T(8,128)(2,1)S(1)}, bf16[144,512]{1,0:T(8,128)(2,1)S(1)}, u32[]{:S(2)}, u32[]{:S(2)}) collective-permute-start(bf16[144,512]{1,0:T(8,128)(2,1)S(1)} %get-tuple-element.28), channel_id=1, source_target_pairs={{0,6},{2,0},{4,2},{6,4},{1,7},{3,1},{5,3},{7,5},{8,14},{10,8},{12,... | collective-permute-start | bytes 442376 | tf_op jit(solution)/shard_map/ppermute | solution.py:26
  104.8 5.1 %collective-permute-start.15 = (bf16[144,512]{1,0:T(8,128)(2,1)S(1)}, bf16[144,512]{1,0:T(8,128)(2,1)S(1)}, u32[]{:S(2)}, u32[]{:S(2)}) collective-permute-start(bf16[144,512]{1,0:T(8,128)(2,1)S(1)} %get-tuple-element.29), channel_id=1, source_target_pairs={{0,2},{2,4},{4,6},{6,0},{1,3},{3,5},{5,7},{7,1},{8,10},{10,12},{12... | collective-permute-start | bytes 442376 | tf_op jit(solution)/shard_map/ppermute | solution.py:26
  110.7 1.4 collective-permute-start.16
  113.4 9.6 %all-to-all-start = ((bf16[4,64,128]{2,1,0:T(8,128)(2,1)}), bf16[4,64,128]{2,1,0:T(8,128)(2,1)S(1)}, u32[]{:S(2)}, u32[]{:S(2)}) async-start(bf16[4,64,128]{2,1,0:T(8,128)(2,1)} %shard_map.97), calls=%async_computation | async-start | bytes 131072 | tf_op jit(solution)/shard_map/all_to_all | solution.py:384
  117.4 31.3 %copy-start.3 = (bf16[8,4096]{1,0:T(8,128)(2,1)S(1)}, bf16[8,4096]{1,0:T(8,128)(2,1)}, u32[]{:S(2)}) copy-start(bf16[8,4096]{1,0:T(8,128)(2,1)} %hidden_ref.1) | copy-start | bytes 196612
  117.4 31.3 %copy-start.5 = (f32[4096]{0:T(1024)S(1)}, f32[4096]{0:T(1024)}, u32[]{:S(2)}) copy-start(f32[4096]{0:T(1024)} %param.15) | copy-start | bytes 49156
  126.9 21.8 %all-to-all-start.1 = ((bf16[8,8,4096]{2,1,0:T(8,128)(2,1)}), bf16[8,8,4096]{2,1,0:T(8,128)(2,1)S(1)}, u32[]{:S(2)}, u32[]{:S(2)}) async-start(bf16[8,8,4096]{2,1,0:T(8,128)(2,1)} %shard_map.98), calls=%async_computation.1 | async-start | bytes 1048576 | tf_op jit(solution)/shard_map/all_to_all | solution.py:384
  132.3 19.9 %collective-permute-start.36 = (bf16[344,512]{1,0:T(8,128)(2,1)S(1)}, bf16[344,512]{1,0:T(8,128)(2,1)S(1)}, u32[]{:S(2)}, u32[]{:S(2)}) collective-permute-start(bf16[344,512]{1,0:T(8,128)(2,1)S(1)} %copy-done.6), channel_id=1, source_target_pairs={{0,6},{2,0},{4,2},{6,4},{1,7},{3,1},{5,3},{7,5},{8,14},{10,8},{12,... | collective-permute-start | bytes 1056776 | tf_op jit(solution)/shard_map/ppermute | solution.py:26
  135.6 16.7 %collective-permute-start.35 = (bf16[344,512]{1,0:T(8,128)(2,1)S(1)}, bf16[344,512]{1,0:T(8,128)(2,1)S(1)}, u32[]{:S(2)}, u32[]{:S(2)}) collective-permute-start(bf16[344,512]{1,0:T(8,128)(2,1)S(1)} %copy-done.6), channel_id=1, source_target_pairs={{0,4},{2,6},{4,0},{6,2},{1,5},{3,7},{5,1},{7,3},{8,12},{10,14},{12... | collective-permute-start | bytes 1056776 | tf_op jit(solution)/shard_map/ppermute | solution.py:26
  135.7 16.6 %collective-permute-start.34 = (bf16[344,512]{1,0:T(8,128)(2,1)S(1)}, bf16[344,512]{1,0:T(8,128)(2,1)S(1)}, u32[]{:S(2)}, u32[]{:S(2)}) collective-permute-start(bf16[344,512]{1,0:T(8,128)(2,1)S(1)} %copy-done.6), channel_id=1, source_target_pairs={{0,2},{2,4},{4,6},{6,0},{1,3},{3,5},{5,7},{7,1},{8,10},{10,12},{12... | collective-permute-start | bytes 1056776 | tf_op jit(solution)/shard_map/ppermute | solution.py:26
  149.5 4.3 %collective-permute-start.26 = (bf16[8,4096]{1,0:T(8,128)(2,1)S(1)}, bf16[8,4096]{1,0:T(8,128)(2,1)S(1)}, u32[]{:S(2)}, u32[]{:S(2)}) collective-permute-start(bf16[8,4096]{1,0:T(8,128)(2,1)S(1)} %get-tuple-element.37), channel_id=1, source_target_pairs={{0,24},{8,0},{16,8},{24,16},{1,25},{9,1},{17,9},{25,17},{2,26},{10... | collective-permute-start | bytes 196616 | tf_op jit(solution)/shard_map/ppermute | solution.py:26
  150.9 5.8 %collective-permute-start.25 = (bf16[8,4096]{1,0:T(8,128)(2,1)S(1)}, bf16[8,4096]{1,0:T(8,128)(2,1)S(1)}, u32[]{:S(2)}, u32[]{:S(2)}) collective-permute-start(bf16[8,4096]{1,0:T(8,128)(2,1)S(1)} %get-tuple-element.37), channel_id=1, source_target_pairs={{0,16},{8,24},{16,0},{24,8},{1,17},{9,25},{17,1},{25,9},{2,18},{10... | collective-permute-start | bytes 196616 | tf_op jit(solution)/shard_map/ppermute | solution.py:26
  152.3 5.5 %collective-permute-start.24 = (bf16[8,4096]{1,0:T(8,128)(2,1)S(1)}, bf16[8,4096]{1,0:T(8,128)(2,1)S(1)}, u32[]{:S(2)}, u32[]{:S(2)}) collective-permute-start(bf16[8,4096]{1,0:T(8,128)(2,1)S(1)} %get-tuple-element.37), channel_id=1, source_target_pairs={{0,8},{8,16},{16,24},{24,0},{1,9},{9,17},{17,25},{25,1},{2,10},{10... | collective-permute-start | bytes 196616 | tf_op jit(solution)/shard_map/ppermute | solution.py:26
  152.5 46.3 %collective-permute-start.37 = (bf16[4,344,512]{2,1,0:T(8,128)(2,1)S(1)}, bf16[4,344,512]{2,1,0:T(8,128)(2,1)S(1)}, u32[]{:S(2)}, u32[]{:S(2)}) collective-permute-start(bf16[4,344,512]{2,1,0:T(8,128)(2,1)S(1)} %pad_maximum_fusion.1.refs_0_), channel_id=1, source_target_pairs={{0,1},{1,0},{2,3},{3,2},{4,5},{5,4},{6,7},{7,6},{8,9},{9,8},{10,11... | collective-permute-start | bytes 4227080 | tf_op jit(solution)/shard_map/ppermute | solution.py:26
  157.8 8.7 %collective-permute-start.27 = (bf16[32,4096]{1,0:T(8,128)(2,1)S(1)}, bf16[32,4096]{1,0:T(8,128)(2,1)S(1)}, u32[]{:S(2)}, u32[]{:S(2)}) collective-permute-start(bf16[32,4096]{1,0:T(8,128)(2,1)S(1)} %pad_maximum_fusion.3.refs_0_), channel_id=1, source_target_pairs={{0,32},{32,64},{64,96},{96,128},{128,160},{160,192},{192,224},{224... | collective-permute-start | bytes 786440 | tf_op jit(solution)/shard_map/ppermute | solution.py:26
  158.4 8.1 %collective-permute-start.28 = (bf16[32,4096]{1,0:T(8,128)(2,1)S(1)}, bf16[32,4096]{1,0:T(8,128)(2,1)S(1)}, u32[]{:S(2)}, u32[]{:S(2)}) collective-permute-start(bf16[32,4096]{1,0:T(8,128)(2,1)S(1)} %pad_maximum_fusion.3.refs_0_), channel_id=1, source_target_pairs={{0,224},{32,0},{64,32},{96,64},{128,96},{160,128},{192,160},{224,1... | collective-permute-start | bytes 786440 | tf_op jit(solution)/shard_map/ppermute | solution.py:26
  166.5 9.8 %collective-permute-start.29 = (bf16[32,4096]{1,0:T(8,128)(2,1)S(1)}, bf16[32,4096]{1,0:T(8,128)(2,1)S(1)}, u32[]{:S(2)}, u32[]{:S(2)}) collective-permute-start(bf16[32,4096]{1,0:T(8,128)(2,1)S(1)} %collective-permute-done.27.refs_1_), channel_id=1, source_target_pairs={{0,32},{32,64},{64,96},{96,128},{128,160},{160,192},{192,224},{224... | collective-permute-start | bytes 786440 | tf_op jit(solution)/shard_map/ppermute | solution.py:26
  166.5 9.9 %collective-permute-start.30 = (bf16[32,4096]{1,0:T(8,128)(2,1)S(1)}, bf16[32,4096]{1,0:T(8,128)(2,1)S(1)}, u32[]{:S(2)}, u32[]{:S(2)}) collective-permute-start(bf16[32,4096]{1,0:T(8,128)(2,1)S(1)} %collective-permute-done.28.refs_2_), channel_id=1, source_target_pairs={{0,224},{32,0},{64,32},{96,64},{128,96},{160,128},{192,160},{224,1... | collective-permute-start | bytes 786440 | tf_op jit(solution)/shard_map/ppermute | solution.py:26
  176.3 9.8 %collective-permute-start.31 = (bf16[32,4096]{1,0:T(8,128)(2,1)S(1)}, bf16[32,4096]{1,0:T(8,128)(2,1)S(1)}, u32[]{:S(2)}, u32[]{:S(2)}) collective-permute-start(bf16[32,4096]{1,0:T(8,128)(2,1)S(1)} %collective-permute-done.29.refs_3_), channel_id=1, source_target_pairs={{0,32},{32,64},{64,96},{96,128},{128,160},{160,192},{192,224},{224... | collective-permute-start | bytes 786440 | tf_op jit(solution)/shard_map/ppermute | solution.py:26
  176.4 9.7 %collective-permute-start.32 = (bf16[32,4096]{1,0:T(8,128)(2,1)S(1)}, bf16[32,4096]{1,0:T(8,128)(2,1)S(1)}, u32[]{:S(2)}, u32[]{:S(2)}) collective-permute-start(bf16[32,4096]{1,0:T(8,128)(2,1)S(1)} %collective-permute-done.30.refs_4_), channel_id=1, source_target_pairs={{0,224},{32,0},{64,32},{96,64},{128,96},{160,128},{192,160},{224,1... | collective-permute-start | bytes 786440 | tf_op jit(solution)/shard_map/ppermute | solution.py:26
  186.1 7.6 %collective-permute-start.33 = (bf16[32,4096]{1,0:T(8,128)(2,1)S(1)}, bf16[32,4096]{1,0:T(8,128)(2,1)S(1)}, u32[]{:S(2)}, u32[]{:S(2)}) collective-permute-start(bf16[32,4096]{1,0:T(8,128)(2,1)S(1)} %collective-permute-done.31.refs_5_), channel_id=1, source_target_pairs={{0,32},{32,64},{64,96},{96,128},{128,160},{160,192},{192,224},{224... | collective-permute-start | bytes 786440 | tf_op jit(solution)/shard_map/ppermute | solution.py:26
  201.9 11.5 %collective-permute-start.38 = (bf16[64,4096]{1,0:T(8,128)(2,1)S(1)}, bf16[64,4096]{1,0:T(8,128)(2,1)S(1)}, u32[]{:S(2)}, u32[]{:S(2)}) collective-permute-start(bf16[64,4096]{1,0:T(8,128)(2,1)S(1)} %get-tuple-element.40), channel_id=1, source_target_pairs={{0,24},{8,0},{16,8},{24,16},{1,25},{9,1},{17,9},{25,17},{2,26},{10... | collective-permute-start | bytes 1572872 | tf_op jit(solution)/shard_map/ppermute | solution.py:26
  202.0 13.1 %collective-permute-start.39 = (bf16[64,4096]{1,0:T(8,128)(2,1)S(1)}, bf16[64,4096]{1,0:T(8,128)(2,1)S(1)}, u32[]{:S(2)}, u32[]{:S(2)}) collective-permute-start(bf16[64,4096]{1,0:T(8,128)(2,1)S(1)} %get-tuple-element.41), channel_id=1, source_target_pairs={{0,16},{8,24},{16,0},{24,8},{1,17},{9,25},{17,1},{25,9},{2,18},{10... | collective-permute-start | bytes 1572872 | tf_op jit(solution)/shard_map/ppermute | solution.py:26
  202.1 18.5 %collective-permute-start.40 = (bf16[64,4096]{1,0:T(8,128)(2,1)S(1)}, bf16[64,4096]{1,0:T(8,128)(2,1)S(1)}, u32[]{:S(2)}, u32[]{:S(2)}) collective-permute-start(bf16[64,4096]{1,0:T(8,128)(2,1)S(1)} %get-tuple-element.42), channel_id=1, source_target_pairs={{0,8},{8,16},{16,24},{24,0},{1,9},{9,17},{17,25},{25,1},{2,10},{10... | collective-permute-start | bytes 1572872 | tf_op jit(solution)/shard_map/ppermute | solution.py:26
  (3 other events, 51.6 us)
